TPU v7x, 32 devices: a whole 2x2x4 slice. The times are simulated.
32 devices in a mesh: group: 8 (over z, core), member: 4 (over y, x).
Axes of the slice: x: 2, y: 2, z: 4, core: 2. Of those that a mesh axis runs over, the one named last changes fastest.
Arguments:
- rhs: bfloat16 [8, 4, 768, 128], P('group', 'member'), may hold values from -6 to 6
- leaf_pivot_inverse: bfloat16 [8, 4, 768, 768], P('group', 'member'), may hold values from -1.5 to 1.5, as said below
- leaf_border_block: bfloat16 [8, 4, 512, 768], P('group', 'member'), may hold values from -0.21875 to 0.21875
- leaf_map: int32 [8, 4, 4], P('group'), may hold values from 0 to 47, as said below
- mid_inverse: bfloat16 [8, 2048, 2048], P('group', 'member'), may hold values from -1.5 to 1.5, as said below
- mid_border: bfloat16 [8, 4096, 2048], P('group', None, 'member'), may hold values from -0.125 to 0.125
- root_map: int32 [8, 4, 8], P('group', 'member'), may hold values from 0 to 15, as said below
- root_inverse: bfloat16 [8192, 8192], P('group', 'member'), may hold values from -0.5 to 0.5, as said below
Outputs:
- leaf_solution: bfloat16 [8, 4, 768, 128], P('group', 'member')
- mid_solution: bfloat16 [8, 2048, 128], P('group', 'member')
- root_solution: bfloat16 [4, 2048, 128], P('member', 'group')
Inputs may be any that keep to these rules, and one draw needn't show every extreme that they name: `leaf_map`: for each (g, m) the 4 entries are distinct; a value k below 16 names pivot block k of the mid-level front, a larger one border block k - 16. `root_map`: for each (g, m) the entries are distinct. `leaf_pivot_inverse`: each [768, 768] matrix is lower triangular with a positive diagonal, as the inverse of a Cholesky factor is: every entry above the diagonal is zero. `mid_inverse`: each [2048, 2048] matrix is lower triangular with a positive diagonal, as the inverse of a Cholesky factor is: every entry above the diagonal is zero. `root_inverse`: lower triangular with a positive diagonal, as the inverse of a Cholesky factor is: every entry above the diagonal is zero.
All inputs are finite; a program needn't handle non-finite values.
Results may differ from a plain program's by a relative error of at most 0.028.
Values may be sent and summed in bfloat16 or wider, within the bound.
No kernel may reach another device: no remote copies, remote signals or barrier semaphores. Data moves between devices by JAX's collectives and lax.ppermute only.
A program may use at most 64 MiB of HBM per device.

v0:
```python
import functools

import jax
import jax.numpy as jnp
from jax import lax
from jax.experimental import pallas as pl
from jax.experimental.pallas import tpu as pltpu
from jax.sharding import PartitionSpec as P


BLOCK = 128
VMEM_LIMIT = 20 * 1024 * 1024
PREFETCH_FLOPS = 2 * 10**10
SHARE_FLOPS = 2 * 10**8
F32 = jnp.float32
BF16 = jnp.bfloat16


def is_power_of_two(size):
    return size & (size - 1) == 0


def partner(index, step, size):
    return index ^ step if is_power_of_two(size) else (index + step) % size


def exchange(values, axis, step, size):
    return lax.ppermute(values, axis, [(i, partner(i, step, size)) for i in range(size)])


def times_transpose(values, matrix):
    return lax.dot_general(values, matrix, (((1,), (1,)), ((), ())), preferred_element_type=F32)


def times(values, matrix):
    return jnp.dot(values, matrix, preferred_element_type=F32)


def traced_source(index, step, size):
    if is_power_of_two(size):
        return lax.bitwise_xor(index, jnp.int32(step))
    return lax.rem(index - step + size, jnp.int32(size))


def traced_partner(index, step, size):
    if is_power_of_two(size):
        return lax.bitwise_xor(index, jnp.int32(step))
    return lax.rem(index + step, jnp.int32(size))


def at_block(index):
    return pl.ds(pl.multiple_of(index * BLOCK, BLOCK), BLOCK)


def at_part(index, size):
    return pl.ds(pl.multiple_of(index * size, BLOCK), size)


def static_block(index):
    return pl.ds(index * BLOCK, BLOCK)


def chunks_of(size):
    rows = 2 * BLOCK if size % (2 * BLOCK) == 0 else size
    return [(first, rows) for first in range(0, size, rows)]


def leaf_forward_kernel(
    rhs_hbm,
    factor_hbm,
    edge_hbm,
    leaf_map_hbm,
    root_map_hbm,
    forward_ref,
    factor_ref,
    edge_ref,
    leaf_map_ref,
    root_map_ref,
    rhs_ref,
    sems,
):
    chunks = chunks_of(factor_ref.shape[0])
    copies = [pltpu.make_async_copy(rhs_hbm.at[0, 0], rhs_ref, sems.at[0])]
    for i, (first, rows) in enumerate(chunks, start=1):
        part = (pl.ds(first, rows), pl.ds(0, first + rows))
        copies.append(
            pltpu.make_async_copy(factor_hbm.at[0, 0, *part], factor_ref.at[*part], sems.at[i])
        )
    later = [
        pltpu.make_async_copy(source_ref, target_ref, sems.at[1 + len(chunks) + i])
        for i, (source_ref, target_ref) in enumerate(
            (
                (edge_hbm.at[0, 0], edge_ref),
                (leaf_map_hbm, leaf_map_ref),
                (root_map_hbm, root_map_ref),
            )
        )
    ]
    for copy in copies + later:
        copy.start()
    copies[0].wait()
    source_rows = rhs_ref[...].T
    for copy, (first, rows) in zip(copies[1:], chunks):
        copy.wait()
        factor = factor_ref[pl.ds(first, rows), pl.ds(0, first + rows)]
        forward = times_transpose(source_rows[:, : first + rows], factor)
        forward_ref[:, pl.ds(first, rows)] = forward.astype(BF16)
    for copy in later:
        copy.wait()


def leaf_out_kernel(forward_ref, edge_ref, out_ref):
    out_ref[...] = (-times_transpose(forward_ref[...], edge_ref[...])).astype(BF16)


def border_piece(border_ref, owner, rows):
    return border_ref[0, pl.ds(pl.multiple_of(owner * rows, BLOCK), rows), :]


def mid_forward_kernel(members, which, map_ref, inverse_ref, *refs):
    forward_ref = refs[-1]
    terms = refs[: len(which)]
    before = refs[len(which) : -1]
    pivot_blocks = inverse_ref.shape[2] // BLOCK
    member = lax.axis_index("member")
    total = before[0][...] if before else None
    for k, term in zip(which, terms):
        owner = traced_source(member, k, members)
        blocks = range(term.shape[1] // BLOCK)
        for first in blocks[::2]:
            values, columns = [], []
            for j in blocks[first : first + 2]:
                target = map_ref[0, owner, j]
                block = term[:, static_block(j)]
                values.append(jnp.where(target < pivot_blocks, block, jnp.zeros_like(block)))
                columns.append(inverse_ref[0, :, at_block(lax.min(target, pivot_blocks - 1))])
            part = times_transpose(
                jnp.concatenate(values, axis=1), jnp.concatenate(columns, axis=1)
            )
            total = part if total is None else total + part
    forward_ref[...] = total.astype(forward_ref.dtype)


def mid_piece_kernel(members, step, border_ref, forward_ref, low_ref, high_ref):
    owner = traced_partner(lax.axis_index("member"), step, members)
    rows = low_ref.shape[1]
    for half, ref in enumerate((low_ref, high_ref)):
        piece = border_piece(border_ref, 2 * owner + half, rows)
        ref[...] = (-times_transpose(forward_ref[...], piece)).astype(BF16)


def own_update_kernel(members, pivot_blocks, *refs):
    map_ref, border_ref, forward_ref = refs[:3]
    terms = refs[3 : 3 + members]
    update_ref = refs[-1]
    member = lax.axis_index("member")
    rows = update_ref.shape[1]
    piece = border_ref[0, pl.ds(pl.multiple_of(member * rows, BLOCK), rows), :]
    update_ref[...] = -times_transpose(forward_ref[...], piece)
    first = pivot_blocks + member * (rows // BLOCK)
    for k, term in enumerate(terms):
        owner = traced_source(member, k, members)
        for j in range(term.shape[1] // BLOCK):
            target = map_ref[0, owner, j] - first

            @pl.when((target >= 0) & (target < rows // BLOCK))
            def _():
                update_ref[:, at_block(target)] += term[:, static_block(j)].astype(F32)


DISTANCES = (0, 2, 1, 3)


def is_split(chips):
    return chips == len(DISTANCES)


def stream_places(core, chips, share):
    if not is_split(chips):
        return [[core * (share // 2)]], share // 2
    chip = lax.axis_index("group") // 2
    size = share // (4 * chips)
    owners = [2 * lax.bitwise_xor(chip, jnp.int32(k)) + core for k in DISTANCES]
    return [[(2 * owner + stream) * size for owner in owners] for stream in range(2)], size


def unit_places(core, chips, share):
    streams, size = stream_places(core, chips, share)
    if not is_split(chips):
        return streams, size
    return [places[i : i + 2] for places in streams for i in (0, 2)], size


def at_places(ref, lines, places, size):
    parts = [ref[lines, pl.ds(pl.multiple_of(place, BLOCK), size)] for place in places]
    return parts[0] if len(parts) == 1 else jnp.concatenate(parts, axis=1)


def take_streams(refs, spread, core, chips):
    streams, size = stream_places(core, chips, spread.shape[1])
    for ref, places in zip(refs, streams):
        for i, place in enumerate(places):
            ref[:, pl.ds(i * size, size)] = spread[:, pl.ds(pl.multiple_of(place, BLOCK), size)]


def root_term_kernel(chips, lows, *refs):
    count = 2 if is_split(chips) else 1
    inputs, outs, spread = refs[: -1 - 2 * count], refs[-1 - 2 * count : -1], refs[-1]
    map_ref, own_ref = inputs[:2]
    arrived = (inputs[2 : 2 + lows], inputs[2 + lows :])
    core = lax.axis_index("group") & 1
    spread[...] = jnp.zeros_like(spread)
    half_blocks = own_ref.shape[1] // (2 * BLOCK)
    for i in range(2 * half_blocks):
        total = own_ref[:, static_block(i)]
        for term in arrived[i // half_blocks]:
            total = total + term[:, static_block(i % half_blocks)].astype(F32)
        spread[:, at_block(map_ref[0, 0, i])] = total.astype(BF16)
    take_streams(outs[:count], spread, 1 - core, chips)
    take_streams(outs[count:], spread, core, chips)


def join(joined, units, chips):
    core = lax.axis_index("group") & 1
    count = len(units) // 2
    for owner, refs in ((core, units[:count]), (1 - core, units[count:])):
        places_of, size = unit_places(owner, chips, joined.shape[1])
        for ref, places in zip(refs, places_of):
            for i, place in enumerate(places):
                target = pl.ds(pl.multiple_of(place, BLOCK), size)
                joined[:, target] = ref[:, pl.ds(i * size, size)]


def root_product(chips, which, units, inverse_ref, lines):
    core = lax.axis_index("group") & 1
    total = None
    for (own, number), ref in zip(which, units):
        places_of, size = unit_places(core if own else 1 - core, chips, inverse_ref.shape[1])
        columns = at_places(inverse_ref, lines, places_of[number], size)
        part = times_transpose(ref[...], columns)
        total = part if total is None else total + part
    return total


def root_early_kernel(chips, which, inverse_ref, *refs):
    units, before, outs = refs[: len(which)], refs[len(which) : -2], refs[-2:]
    rows = outs[0].shape[1]
    for part, out_ref in enumerate(outs):
        total = root_product(chips, which, units, inverse_ref, pl.ds(part * rows, rows))
        out_ref[...] = total + before[part][...] if before else total


def root_forward_kernel(chips, which, part, inverse_ref, *refs):
    units, before_ref, out_ref = refs[:-2], refs[-2], refs[-1]
    rows = out_ref.shape[1]
    total = root_product(chips, which, units, inverse_ref, pl.ds(part * rows, rows))
    out_ref[...] = (total + before_ref[...]).astype(BF16)


def root_back_kernel(chips, owners, part, inverse_ref, forward_ref, *refs):
    count = len(owners) * (2 if is_split(chips) else 1)
    before, outs = refs[:-count], refs[-count:]
    core = lax.axis_index("group") & 1
    places_of = []
    for own in owners:
        streams, size = stream_places(core if own else 1 - core, chips, inverse_ref.shape[1])
        places_of += streams
    forward = forward_ref[...]
    lines = pl.ds(part * forward.shape[1], forward.shape[1])
    for i, (places, out_ref) in enumerate(zip(places_of, outs)):
        total = times(forward, at_places(inverse_ref, lines, places, size))
        if before:
            total = total + before[i][...]
        out_ref[...] = total.astype(out_ref.dtype)


def root_pick_kernel(chips, map_ref, *refs):
    units, (low_ref, high_ref, joined) = refs[:-3], refs[-3:]
    join(joined, units, chips)
    blocks = low_ref.shape[1] // BLOCK
    for i in range(2 * blocks):
        ref = (low_ref, high_ref)[i // blocks]
        ref[:, static_block(i % blocks)] = joined[:, at_block(map_ref[0, 0, i])]


def root_out_kernel(low_ref, high_ref, out_ref):
    rows = out_ref.shape[1] // 2
    for i, ref in enumerate((low_ref, high_ref)):
        out_ref[0, pl.ds(i * rows, rows), :] = ref[:, pl.ds(0, rows)].T


def root_slice_kernel(mine_ref, other_ref, out_ref, joined, turned):
    join(joined, (mine_ref, other_ref), 1)
    rows_out = out_ref.shape[1]
    first = lax.axis_index("group") * rows_out
    rows = turned.shape[0]
    turned[...] = joined[:, at_part(first // rows, rows)].astype(F32).T
    begin = pl.multiple_of(lax.rem(first, jnp.int32(rows)), min(rows_out, rows))
    out_ref[0] = turned[pl.ds(begin, rows_out), :].astype(BF16)


def border_product(members, values, which, border_ref):
    member = lax.axis_index("member")
    total = None
    for (step, half), ref in zip(which, values):
        owner = traced_source(member, step, members)
        piece = border_piece(border_ref, 2 * owner + half, ref.shape[1])
        part = times(ref[...], piece)
        total = part if total is None else total + part
    return total


def mid_early_kernel(members, which, border_ref, back_ref, *refs):
    product = border_product(members, refs[:-1], which, border_ref)
    refs[-1][...] = back_ref[...].astype(F32) - product


def ask(map_ref, owner, part_ref, out_ref):
    pivot_blocks = part_ref.shape[1] // BLOCK
    for j in range(out_ref.shape[1] // BLOCK):
        target = map_ref[0, owner, j]
        block = part_ref[:, at_block(lax.min(target, pivot_blocks - 1))]
        out_ref[:, static_block(j)] = jnp.where(
            target < pivot_blocks, block, jnp.zeros_like(block)
        )


def mid_back_kernel(members, late, map_ref, inverse_ref, border_ref, back_ref, *refs):
    values = refs[:-3]
    part_ref, asked_ref, piece_ref = refs[-3:]
    back = back_ref[...] - border_product(members, values, late, border_ref)
    part_ref[...] = times(back.astype(BF16), inverse_ref[0]).astype(BF16)
    owner = traced_partner(lax.axis_index("member"), members - 1, members)
    ask(map_ref, owner, part_ref, asked_ref)
    piece_ref[...] = part_ref[:, at_part(owner, piece_ref.shape[1])]


def mid_share_kernel(members, step, map_ref, part_ref, asked_ref, piece_ref):
    owner = traced_partner(lax.axis_index("member"), step, members)
    ask(map_ref, owner, part_ref, asked_ref)
    piece_ref[...] = part_ref[:, at_part(owner, piece_ref.shape[1])]


def pick_kernel(members, map_ref, part_ref, *refs):
    values = refs[:-2]
    base_ref, own_ref = refs[-2:]
    member = lax.axis_index("member")
    pivot_blocks = part_ref.shape[1] // BLOCK
    rows = values[0].shape[1]
    for j in range(base_ref.shape[1] // BLOCK):
        target = map_ref[0, member, j]

        @pl.when(target < pivot_blocks)
        def _():
            base_ref[:, static_block(j)] = part_ref[:, at_block(target)]

        border = target - pivot_blocks
        for k, values_ref in enumerate(values):
            owner = traced_source(member, k // 2, members)
            inner = border - (2 * owner + k % 2) * (rows // BLOCK)

            @pl.when((border >= 0) & (inner >= 0) & (inner < rows // BLOCK))
            def _():
                base_ref[:, static_block(j)] = values_ref[:, at_block(inner)]

    own_ref[...] = part_ref[:, at_part(member, own_ref.shape[1])]


def leaf_back_kernel(*refs):
    factor_ref, edge_ref, forward_ref = refs[:3]
    terms = refs[3:-1]
    out_ref = refs[-1]
    picked = terms[0][...].astype(F32)
    for term in terms[1:]:
        picked = picked + term[...].astype(F32)
    back = forward_ref[...].astype(F32) - times(picked.astype(BF16), edge_ref[...])
    back = back.astype(BF16)
    chunks = chunks_of(factor_ref.shape[0])
    for first, rows in chunks:
        total = None
        for lower, size in chunks:
            if lower >= first:
                factor = factor_ref[pl.ds(lower, size), pl.ds(first, rows)]
                part = times(back[:, lower : lower + size], factor)
                total = part if total is None else total + part
        out_ref[0, 0, pl.ds(first, rows), :] = total.astype(BF16).T


def mid_out_kernel(*refs):
    total = refs[0][...].astype(F32)
    for term in refs[1:-1]:
        total = total + term[...].astype(F32)
    refs[-1][0] = total.astype(BF16).T


def call(kernel, inputs, outs, scratch=(), flops=0, space=pltpu.VMEM):
    vmem = pl.BlockSpec(memory_space=pltpu.VMEM)
    smem = pl.BlockSpec(memory_space=pltpu.SMEM)
    in_specs = [smem if x.dtype == jnp.int32 else vmem for x in inputs]
    out_shape = [jax.ShapeDtypeStruct(shape, dtype) for shape, dtype in outs]
    if space == pltpu.HBM:
        in_specs = [pl.BlockSpec(memory_space=space)] * len(inputs)
        inputs = [pltpu.with_memory_space_constraint(x, space) for x in inputs]
        out_shape = [
            (pltpu.SMEM if dtype == jnp.int32 else pltpu.VMEM)(shape, dtype)
            for shape, dtype in outs
        ]
    moved = sum(x.size * x.dtype.itemsize for x in inputs)
    return pl.pallas_call(
        kernel,
        in_specs=in_specs,
        out_specs=[smem if dtype == jnp.int32 else vmem for _, dtype in outs],
        out_shape=out_shape,
        scratch_shapes=list(scratch),
        compiler_params=pltpu.CompilerParams(vmem_limit_bytes=VMEM_LIMIT),
        cost_estimate=pl.CostEstimate(flops=flops, bytes_accessed=moved, transcendentals=0),
    )(*inputs)


def total_of(first, others):
    total = first.astype(F32)
    for other in others:
        total = total + other.astype(F32)
    return total.astype(BF16)


def chips_of(groups, rows_out):
    chips = groups // 2
    return chips if is_split(chips) and rows_out % (2 * BLOCK) == 0 else 1


def group_sum(mine, other, size, chips):
    if not is_split(chips):
        total = total_of(mine[0], [exchange(other[0], "group", 1, size)])
        total = total_of(total, [exchange(total, "group", k, size) for k in range(2, size, 2)])
        return [total], [exchange(total, "group", 1, size)]
    own_units, other_units = [], []
    for kept, given in zip(mine, other):
        rows = kept.shape[1] // 2
        block = rows // 2
        low, high = split(kept, rows)
        low_core, high_core = split(exchange(given, "group", 1, size), rows)
        pair = exchange(total_of(high, [high_core]), "group", 2, size)
        side = total_of(low, [low_core, pair])
        far, near = split(exchange(side, "group", 4, size), block)
        unit = total_of(side, [jnp.concatenate([near, far], axis=1)])
        rest = exchange(unit, "group", 2, size)
        own_units += [unit, rest]
        other_units += [exchange(unit, "group", 1, size), exchange(rest, "group", 1, size)]
    return own_units, other_units


def member_sum(low, high, size):
    if not is_power_of_two(size):
        return lax.psum(low, "member"), lax.psum(high, "member")
    steps = [1 << i for i in range(size.bit_length() - 1)]
    for first, second in zip(steps, reversed(steps)):
        other_low = exchange(low, "member", first, size)
        other_high = exchange(high, "member", second, size)
        low, high = total_of(low, [other_low]), total_of(high, [other_high])
    return low, high


def split(values, rows):
    return values[:, :rows], values[:, rows:]


def scatter_sum(pieces, size):
    rows = pieces[0][0].shape[1]
    if size != 4:
        arrived = [
            split(exchange(jnp.concatenate(pair, axis=1), "member", k, size), rows)
            for k, pair in enumerate(pieces, start=1)
        ]
        return [low for low, _ in arrived], [high for _, high in arrived]
    (low1, high1), (low2, high2), (low3, high3) = pieces
    relay1 = exchange(low3, "member", 1, size)
    relay2 = exchange(high3, "member", 2, size)
    first1 = exchange(low1, "member", 1, size)
    first2 = exchange(high2, "member", 2, size)
    last2 = exchange(total_of(low2, [relay1]), "member", 2, size)
    last1 = exchange(total_of(high1, [relay2]), "member", 1, size)
    return [first1, last2], [first2, last1]


def gather(low, high, size):
    rows = low.shape[1]
    if size != 4:
        values = jnp.concatenate([low, high], axis=1)
        return [(low, high)] + [
            split(exchange(values, "member", k, size), rows) for k in range(1, size)
        ]
    high1 = exchange(high, "member", 1, size)
    low2 = exchange(low, "member", 2, size)
    low1 = exchange(low, "member", 1, size)
    high2 = exchange(high, "member", 2, size)
    low3 = exchange(low2, "member", 1, size)
    high3 = exchange(high1, "member", 2, size)
    return [(low, high), (low1, high1), (low2, high2), (low3, high3)]


def make_on_device(groups, members):
    steps = range(1, members)

    def on_device(
        rhs,
        leaf_pivot_inverse,
        leaf_border_block,
        leaf_map,
        mid_inverse,
        mid_border,
        root_map,
        root_inverse,
    ):
        columns = rhs.shape[3]
        leaf_pivots = rhs.shape[2]
        leaf_rows = leaf_border_block.shape[2]
        own_pivots, pivots = mid_inverse.shape[1:]
        border_rows = mid_border.shape[1]
        own_border = border_rows // members
        row_count, share_rows = root_inverse.shape
        half = share_rows // 2
        rows_out = share_rows // groups

        def flat(rows, dtype=BF16):
            return ((columns, rows), dtype)

        def spread_over_members(values):
            return [values] + [exchange(values, "member", k, members) for k in steps]

        leaf_forward, leaf_factor, leaf_edge, leaf_map, root_map = call(
            leaf_forward_kernel,
            [rhs, leaf_pivot_inverse, leaf_border_block, leaf_map, root_map],
            [
                flat(leaf_pivots),
                (leaf_pivot_inverse.shape[2:], BF16),
                (leaf_border_block.shape[2:], BF16),
                (leaf_map.shape, jnp.int32),
                (root_map.shape, jnp.int32),
            ],
            [
                pltpu.VMEM((leaf_pivots, columns), BF16),
                pltpu.SemaphoreType.DMA((4 + len(chunks_of(leaf_pivots)),)),
            ],
            flops=2 * columns * leaf_pivots * leaf_pivots,
            space=pltpu.HBM,
        )
        (leaf_out,) = call(
            leaf_out_kernel, [leaf_forward, leaf_edge], [flat(leaf_rows)], flops=PREFETCH_FLOPS
        )
        terms = spread_over_members(leaf_out)
        mid_forward = []
        groups_of_terms = [[0], list(steps)]
        if members == 4:
            groups_of_terms = [[0], [3], [2, 1]]
        for which in groups_of_terms:
            last = which is groups_of_terms[-1]
            mid_forward = call(
                functools.partial(mid_forward_kernel, members, which),
                [leaf_map, mid_inverse, *(terms[k] for k in which), *mid_forward],
                [flat(own_pivots, BF16 if last else F32)],
                flops=2 * columns * own_pivots * leaf_rows * len(which),
            )
        (mid_forward,) = mid_forward
        half_border = own_border // 2
        pieces = {
            k: call(
                functools.partial(mid_piece_kernel, members, k),
                [mid_border, mid_forward],
                [flat(half_border), flat(half_border)],
                flops=2 * columns * own_pivots * own_border,
            )
            for k in reversed(steps)
        }
        lows, highs = scatter_sum([pieces[k] for k in steps], members)
        (own_update,) = call(
            functools.partial(own_update_kernel, members, pivots // BLOCK),
            [leaf_map, mid_border, mid_forward, *terms],
            [flat(own_border, F32)],
            flops=2 * columns * own_pivots * own_border,
        )
        chips = chips_of(groups, rows_out)
        whole_share = pltpu.VMEM((columns, share_rows), BF16)
        half_streams = [flat(half // 2)] * 2 if is_split(chips) else [flat(half)]
        count = len(half_streams)
        streams = call(
            functools.partial(root_term_kernel, chips, len(lows)),
            [root_map, own_update, *lows, *highs],
            half_streams * 2,
            [whole_share],
        )
        units = group_sum(streams[count:], streams[:count], groups, chips)
        if is_split(chips):
            waves = [
                [(1, 0), (1, 2)],
                [(0, 0), (0, 2), (1, 1)],
                [(1, 3), (0, 1)],
                [(0, 3)],
            ]
        else:
            waves = [[(1, 0)], [(0, 0)]]
        root_flops = columns * row_count * share_rows
        half_count = row_count // 2
        before = []
        for which in waves[:-1]:
            before = call(
                functools.partial(root_early_kernel, chips, which),
                [root_inverse, *(units[1 - own][k] for own, k in which), *before],
                [flat(half_count, F32), flat(half_count, F32)],
                flops=root_flops // 2,
            )
        root_parts = [
            call(
                functools.partial(root_forward_kernel, chips, waves[-1], part),
                [root_inverse, *(units[1 - own][k] for own, k in waves[-1]), total],
                [flat(half_count)],
                flops=root_flops // 4,
            )[0]
            for part, total in enumerate(before)
        ]
        root_forward = member_sum(*root_parts, members)
        first = call(
            functools.partial(root_back_kernel, chips, (0, 1), 0),
            [root_inverse, root_forward[0]],
            [(shape, F32) for shape, _ in half_streams * 2],
            flops=root_flops,
        )
        other, mine = (
            call(
                functools.partial(root_back_kernel, chips, (own,), 1),
                [root_inverse, root_forward[1], *first[own * count : (own + 1) * count]],
                half_streams,
                flops=root_flops // 2,
            )
            for own in (0, 1)
        )
        mine, other = group_sum(mine, other, groups, chips)
        own_values = call(
            functools.partial(root_pick_kernel, chips),
            [root_map, *mine, *other],
            [flat(half_border), flat(half_border)],
            [whole_share],
        )
        shape = [((1, rows_out, columns), BF16)]
        if is_split(chips):
            (root_out,) = call(root_out_kernel, [mine[0], mine[2]], shape)
        else:
            turned = pltpu.VMEM((max(rows_out, BLOCK), columns), F32)
            (root_out,) = call(root_slice_kernel, [*mine, *other], shape, [whole_share, turned])
        values = gather(*own_values, members)
        if members == 4:
            waves = [[(0, 0), (0, 1), (1, 1), (2, 0)], [(1, 0), (2, 1)], [(3, 0), (3, 1)]]
        else:
            waves = [[(0, 0), (0, 1)], [(k, h) for k in steps for h in range(2)]]
        back = mid_forward
        for which in waves[:-1]:
            (back,) = call(
                functools.partial(mid_early_kernel, members, which),
                [mid_border, back] + [values[k][h] for k, h in which],
                [flat(own_pivots, F32)],
                flops=2 * columns * own_pivots * half_border * len(which),
            )
        part, *last_pair = call(
            functools.partial(mid_back_kernel, members, waves[-1]),
            [leaf_map, mid_inverse, mid_border, back] + [values[k][h] for k, h in waves[-1]],
            [flat(pivots), flat(leaf_rows), flat(own_pivots)],
            flops=2 * columns * own_pivots * (pivots + half_border * len(waves[-1])),
        )
        pairs = [
            call(
                functools.partial(mid_share_kernel, members, k),
                [leaf_map, part],
                [flat(leaf_rows), flat(own_pivots)],
                flops=SHARE_FLOPS,
            )
            for k in steps[:-1]
        ]
        picked, pieces = scatter_sum([*pairs, last_pair], members)
        base, own_piece = call(
            functools.partial(pick_kernel, members),
            [leaf_map, part] + [half for pair in values for half in pair],
            [flat(leaf_rows), flat(own_pivots)],
            flops=SHARE_FLOPS,
        )
        (leaf_values,) = call(
            leaf_back_kernel,
            [leaf_factor, leaf_edge, leaf_forward, base, *picked],
            [((1, 1, leaf_pivots, columns), BF16)],
            flops=2 * columns * leaf_pivots * (leaf_pivots + leaf_rows),
        )
        (mid_out,) = call(mid_out_kernel, [own_piece, *pieces], [((1, own_pivots, columns), BF16)])
        return leaf_values, mid_out, root_out

    return on_device


def solution(mesh):
    in_specs = (
        P("group", "member", None, None),
        P("group", "member", None, None),
        P("group", "member", None, None),
        P("group", None, None),
        P("group", "member", None),
        P("group", None, "member"),
        P("group", "member", None),
        P("group", "member"),
    )
    out_specs = (
        P("group", "member", None, None),
        P("group", "member", None),
        P("member", "group", None),
    )
    on_device = make_on_device(mesh.shape["group"], mesh.shape["member"])

    return jax.shard_map(
        on_device, mesh=mesh, in_specs=in_specs, out_specs=out_specs, check_vma=False
    )
```

profile of v0, /device:TPU:0, one launch (start us, length us, event | category | flops | bytes accessed | tf_op | source)
XLA Modules:
  0.0 109.9 jit_solution(7870287661453353230)
XLA Ops:
  0.6 2.0 %shard_map.103 = (bf16[128,768]{1,0:T(8,128)(2,1)S(1)}, bf16[768,768]{1,0:T(8,128)(2,1)S(1)}, bf16[512,768]{1,0:T(8,128)(2,1)S(1)}, s32[1,4,4]{2,1,0:T(4,128)S(4)}, s32[1,1,8]{2,1,0:T(1,128)S(4)}) custom-call(bf16[1,1,768,128]{3,2,1,0:T(8,128)(2,1)} %rhs_hbm.1, bf16[1,1,768,768]{3,2,1,0:T(8,128)(2,1)} %factor_hbm.1, bf16[1,1,512,768]{3,2,1,0:T(8,128)(2,1)} %edge_hbm.1, ...), custom_call_target="tpu_custom_call" | custom-call | flops 150994944 | bytes 2162784 | tf_op jit(solution)/shard_map/pallas_call | solution.py:409
  3.0 4.0 %collective-permute-start.2 = (bf16[128,512]{1,0:T(8,128)(2,1)S(1)}, bf16[128,512]{1,0:T(8,128)(2,1)S(1)}, u32[]{:S(2)}, u32[]{:S(2)}) collective-permute-start(bf16[128,512]{1,0:T(8,128)(2,1)S(1)} %shard_map.104.refs_0_.refs_3_), channel_id=1, source_target_pairs={{0,3},{1,2},{2,1},{3,0},{4,7},{5,6},{6,5},{7,4},{8,11},{9,10},{10,... | collective-permute-start | bytes 393224 | tf_op jit(solution)/shard_map/ppermute | solution.py:28
  8.0 3.4 %collective-permute-done.2.refs_0_.refs_6_ = bf16[128,512]{1,0:T(8,128)(2,1)S(1)} collective-permute-done((bf16[128,512]{1,0:T(8,128)(2,1)S(1)}, bf16[128,512]{1,0:T(8,128)(2,1)S(1)}, u32[]{:S(2)}, u32[]{:S(2)}) %collective-permute-start.2) | collective-permute-done | bytes 131104 | tf_op jit(solution)/shard_map/ppermute | solution.py:28
  11.7 1.9 %collective-permute-done.1.refs_1_.refs_4_ = bf16[128,512]{1,0:T(8,128)(2,1)S(1)} collective-permute-done((bf16[128,512]{1,0:T(8,128)(2,1)S(1)}, bf16[128,512]{1,0:T(8,128)(2,1)S(1)}, u32[]{:S(2)}, u32[]{:S(2)}) %collective-permute-start.1) | collective-permute-done | bytes 131104 | tf_op jit(solution)/shard_map/ppermute | solution.py:28
  14.6 1.6 %collective-permute-start.4 = (bf16[128,512]{1,0:T(8,128)(2,1)S(1)}, bf16[128,512]{1,0:T(8,128)(2,1)S(1)}, u32[]{:S(2)}, u32[]{:S(2)}) collective-permute-start(bf16[128,512]{1,0:T(8,128)(2,1)S(1)} %get-tuple-element.50), channel_id=1, source_target_pairs={{0,1},{1,0},{2,3},{3,2},{4,5},{5,4},{6,7},{7,6},{8,9},{9,8},{10,11... | collective-permute-start | bytes 393224 | tf_op jit(solution)/shard_map/ppermute | solution.py:28
  19.8 1.8 %collective-permute-start.5 = (bf16[128,512]{1,0:T(8,128)(2,1)S(1)}, bf16[128,512]{1,0:T(8,128)(2,1)S(1)}, u32[]{:S(2)}, u32[]{:S(2)}) collective-permute-start(bf16[128,512]{1,0:T(8,128)(2,1)S(1)} %add_convert_fusion.7), channel_id=1, source_target_pairs={{0,2},{1,3},{2,0},{3,1},{4,6},{5,7},{6,4},{7,5},{8,10},{9,11},{10,... | collective-permute-start | bytes 393224 | tf_op jit(solution)/shard_map/ppermute | solution.py:28
  29.0 1.6 %collective-permute-start.15 = (bf16[128,256]{1,0:T(8,128)(2,1)S(1)}, bf16[128,256]{1,0:T(8,128)(2,1)S(1)}, u32[]{:S(2)}, u32[]{:S(2)}) collective-permute-start(bf16[128,256]{1,0:T(8,128)(2,1)S(1)} %add_convert_fusion.16), channel_id=1, source_target_pairs={{0,8},{4,12},{8,0},{12,4},{16,24},{20,28},{24,16},{28,20},{1,9},{5... | collective-permute-start | bytes 196616 | tf_op jit(solution)/shard_map/ppermute | solution.py:28
  31.2 2.3 %collective-permute-done.15 = bf16[128,256]{1,0:T(8,128)(2,1)S(1)} collective-permute-done((bf16[128,256]{1,0:T(8,128)(2,1)S(1)}, bf16[128,256]{1,0:T(8,128)(2,1)S(1)}, u32[]{:S(2)}, u32[]{:S(2)}) %collective-permute-start.15) | collective-permute-done | bytes 65568 | tf_op jit(solution)/shard_map/ppermute | solution.py:28
  33.5 2.7 %collective-permute-start.16 = (bf16[128,256]{1,0:T(8,128)(2,1)S(1)}, bf16[128,256]{1,0:T(8,128)(2,1)S(1)}, u32[]{:S(2)}, u32[]{:S(2)}) collective-permute-start(bf16[128,256]{1,0:T(8,128)(2,1)S(1)} %add_convert_fusion.15), channel_id=1, source_target_pairs={{0,16},{4,20},{8,24},{12,28},{16,0},{20,4},{24,8},{28,12},{1,17},{... | collective-permute-start | bytes 196616 | tf_op jit(solution)/shard_map/ppermute | solution.py:28
  39.1 2.7 %collective-permute-start.17 = (bf16[128,256]{1,0:T(8,128)(2,1)S(1)}, bf16[128,256]{1,0:T(8,128)(2,1)S(1)}, u32[]{:S(2)}, u32[]{:S(2)}) collective-permute-start(bf16[128,256]{1,0:T(8,128)(2,1)S(1)} %add_convert_fusion.14.refs_0_), channel_id=1, source_target_pairs={{0,8},{4,12},{8,0},{12,4},{16,24},{20,28},{24,16},{28,20},{1,9},{5... | collective-permute-start | bytes 196616 | tf_op jit(solution)/shard_map/ppermute | solution.py:28
  41.8 1.8 %collective-permute-start.12 = (bf16[128,256]{1,0:T(8,128)(2,1)S(1)}, bf16[128,256]{1,0:T(8,128)(2,1)S(1)}, u32[]{:S(2)}, u32[]{:S(2)}) collective-permute-start(bf16[128,256]{1,0:T(8,128)(2,1)S(1)} %add_convert_fusion.17.refs_1_), channel_id=1, source_target_pairs={{0,8},{4,12},{8,0},{12,4},{16,24},{20,28},{24,16},{28,20},{1,9},{5... | collective-permute-start | bytes 196616 | tf_op jit(solution)/shard_map/ppermute | solution.py:28
  44.1 2.0 %collective-permute-done.12.refs_0_ = bf16[128,256]{1,0:T(8,128)(2,1)S(1)} collective-permute-done((bf16[128,256]{1,0:T(8,128)(2,1)S(1)}, bf16[128,256]{1,0:T(8,128)(2,1)S(1)}, u32[]{:S(2)}, u32[]{:S(2)}) %collective-permute-start.12) | collective-permute-done | bytes 65568 | tf_op jit(solution)/shard_map/ppermute | solution.py:28
  49.2 1.6 %collective-permute-start.21 = (bf16[128,512]{1,0:T(8,128)(2,1)S(1)}, bf16[128,512]{1,0:T(8,128)(2,1)S(1)}, u32[]{:S(2)}, u32[]{:S(2)}) collective-permute-start(bf16[128,512]{1,0:T(8,128)(2,1)S(1)} %shard_map.116), channel_id=1, source_target_pairs={{0,2},{1,3},{2,0},{3,1},{4,6},{5,7},{6,4},{7,5},{8,10},{9,11},{10,... | collective-permute-start | bytes 393224 | tf_op jit(solution)/shard_map/ppermute | solution.py:28
  50.9 3.3 %collective-permute-done.23 = bf16[128,512]{1,0:T(8,128)(2,1)S(1)} collective-permute-done((bf16[128,512]{1,0:T(8,128)(2,1)S(1)}, bf16[128,512]{1,0:T(8,128)(2,1)S(1)}, u32[]{:S(2)}, u32[]{:S(2)}) %collective-permute-start.23) | collective-permute-done | bytes 131104 | tf_op jit(solution)/shard_map/ppermute | solution.py:28
  54.2 1.8 %collective-permute-start.24 = (bf16[128,512]{1,0:T(8,128)(2,1)S(1)}, bf16[128,512]{1,0:T(8,128)(2,1)S(1)}, u32[]{:S(2)}, u32[]{:S(2)}) collective-permute-start(bf16[128,512]{1,0:T(8,128)(2,1)S(1)} %add_convert_fusion.3), channel_id=1, source_target_pairs={{0,2},{1,3},{2,0},{3,1},{4,6},{5,7},{6,4},{7,5},{8,10},{9,11},{10,... | collective-permute-start | bytes 393224 | tf_op jit(solution)/shard_map/ppermute | solution.py:28
  56.7 2.7 %collective-permute-done.24 = bf16[128,512]{1,0:T(8,128)(2,1)S(1)} collective-permute-done((bf16[128,512]{1,0:T(8,128)(2,1)S(1)}, bf16[128,512]{1,0:T(8,128)(2,1)S(1)}, u32[]{:S(2)}, u32[]{:S(2)}) %collective-permute-start.24) | collective-permute-done | bytes 131104 | tf_op jit(solution)/shard_map/ppermute | solution.py:28
  63.0 1.9 %collective-permute-start.26 = (bf16[128,256]{1,0:T(8,128)(2,1)S(1)}, bf16[128,256]{1,0:T(8,128)(2,1)S(1)}, u32[]{:S(2)}, u32[]{:S(2)}) collective-permute-start(bf16[128,256]{1,0:T(8,128)(2,1)S(1)} %add_convert_fusion.13), channel_id=1, source_target_pairs={{0,8},{4,12},{8,0},{12,4},{16,24},{20,28},{24,16},{28,20},{1,9},{5... | collective-permute-start | bytes 196616 | tf_op jit(solution)/shard_map/ppermute | solution.py:28
  65.2 2.1 %collective-permute-done.26 = bf16[128,256]{1,0:T(8,128)(2,1)S(1)} collective-permute-done((bf16[128,256]{1,0:T(8,128)(2,1)S(1)}, bf16[128,256]{1,0:T(8,128)(2,1)S(1)}, u32[]{:S(2)}, u32[]{:S(2)}) %collective-permute-start.26) | collective-permute-done | bytes 65568 | tf_op jit(solution)/shard_map/ppermute | solution.py:28
  67.4 4.0 %collective-permute-start.27 = (bf16[128,256]{1,0:T(8,128)(2,1)S(1)}, bf16[128,256]{1,0:T(8,128)(2,1)S(1)}, u32[]{:S(2)}, u32[]{:S(2)}) collective-permute-start(bf16[128,256]{1,0:T(8,128)(2,1)S(1)} %add_convert_fusion.12), channel_id=1, source_target_pairs={{0,16},{4,20},{8,24},{12,28},{16,0},{20,4},{24,8},{28,12},{1,17},{... | collective-permute-start | bytes 196616 | tf_op jit(solution)/shard_map/ppermute | solution.py:28
  72.4 3.3 %collective-permute-done.27 = bf16[128,256]{1,0:T(8,128)(2,1)S(1)} collective-permute-done((bf16[128,256]{1,0:T(8,128)(2,1)S(1)}, bf16[128,256]{1,0:T(8,128)(2,1)S(1)}, u32[]{:S(2)}, u32[]{:S(2)}) %collective-permute-start.27) | collective-permute-done | bytes 65568 | tf_op jit(solution)/shard_map/ppermute | solution.py:28
  78.4 1.6 %collective-permute-done.28.refs_1_ = bf16[128,256]{1,0:T(8,128)(2,1)S(1)} collective-permute-done((bf16[128,256]{1,0:T(8,128)(2,1)S(1)}, bf16[128,256]{1,0:T(8,128)(2,1)S(1)}, u32[]{:S(2)}, u32[]{:S(2)}) %collective-permute-start.28) | collective-permute-done | bytes 65568 | tf_op jit(solution)/shard_map/ppermute | solution.py:28
  87.1 2.3 %collective-permute-done.38.refs_3_.refs_4_ = bf16[128,512]{1,0:T(8,128)(2,1)S(1)} collective-permute-done((bf16[128,512]{1,0:T(8,128)(2,1)S(1)}, bf16[128,512]{1,0:T(8,128)(2,1)S(1)}, u32[]{:S(2)}, u32[]{:S(2)}) %collective-permute-start.38) | collective-permute-done | bytes 131104 | tf_op jit(solution)/shard_map/ppermute | solution.py:28
  97.9 1.6 %collective-permute-start.46 = (bf16[128,512]{1,0:T(8,128)(2,1)S(1)}, bf16[128,512]{1,0:T(8,128)(2,1)S(1)}, u32[]{:S(2)}, u32[]{:S(2)}) collective-permute-start(bf16[128,512]{1,0:T(8,128)(2,1)S(1)} %get-tuple-element.80), channel_id=1, source_target_pairs={{0,2},{1,3},{2,0},{3,1},{4,6},{5,7},{6,4},{7,5},{8,10},{9,11},{10,... | collective-permute-start | bytes 393224 | tf_op jit(solution)/shard_map/ppermute | solution.py:28
  105.0 1.8 %collective-permute-done.48.refs_2_ = bf16[128,512]{1,0:T(8,128)(2,1)S(1)} collective-permute-done((bf16[128,512]{1,0:T(8,128)(2,1)S(1)}, bf16[128,512]{1,0:T(8,128)(2,1)S(1)}, u32[]{:S(2)}, u32[]{:S(2)}) %collective-permute-start.48) | collective-permute-done | bytes 131104 | tf_op jit(solution)/shard_map/ppermute | solution.py:28
  (132 shorter events, 53.3 us)
Async XLA Ops:
  3.0 8.3 %collective-permute-start.2 = (bf16[128,512]{1,0:T(8,128)(2,1)S(1)}, bf16[128,512]{1,0:T(8,128)(2,1)S(1)}, u32[]{:S(2)}, u32[]{:S(2)}) collective-permute-start(bf16[128,512]{1,0:T(8,128)(2,1)S(1)} %shard_map.104.refs_0_.refs_3_), channel_id=1, source_target_pairs={{0,3},{1,2},{2,1},{3,0},{4,7},{5,6},{6,5},{7,4},{8,11},{9,10},{10,... | collective-permute-start | bytes 393224 | tf_op jit(solution)/shard_map/ppermute | solution.py:28
  7.0 6.6 %collective-permute-start.1 = (bf16[128,512]{1,0:T(8,128)(2,1)S(1)}, bf16[128,512]{1,0:T(8,128)(2,1)S(1)}, u32[]{:S(2)}, u32[]{:S(2)}) collective-permute-start(bf16[128,512]{1,0:T(8,128)(2,1)S(1)} %shard_map.104.refs_0_.refs_3_), channel_id=1, source_target_pairs={{0,1},{1,0},{2,3},{3,2},{4,5},{5,4},{6,7},{7,6},{8,9},{9,8},{10,11... | collective-permute-start | bytes 393224 | tf_op jit(solution)/shard_map/ppermute | solution.py:28
  7.5 6.0 %collective-permute-start = (bf16[128,512]{1,0:T(8,128)(2,1)S(1)}, bf16[128,512]{1,0:T(8,128)(2,1)S(1)}, u32[]{:S(2)}, u32[]{:S(2)}) collective-permute-start(bf16[128,512]{1,0:T(8,128)(2,1)S(1)} %shard_map.104.refs_0_.refs_3_), channel_id=1, source_target_pairs={{0,2},{1,3},{2,0},{3,1},{4,6},{5,7},{6,4},{7,5},{8,10},{9,11},{10,... | collective-permute-start | bytes 393224 | tf_op jit(solution)/shard_map/ppermute | solution.py:28
  16.1 6.0 %collective-permute-start.7 = (bf16[128,512]{1,0:T(8,128)(2,1)S(1)}, bf16[128,512]{1,0:T(8,128)(2,1)S(1)}, u32[]{:S(2)}, u32[]{:S(2)}) collective-permute-start(bf16[128,512]{1,0:T(8,128)(2,1)S(1)} %get-tuple-element.53), channel_id=1, source_target_pairs={{0,2},{1,3},{2,0},{3,1},{4,6},{5,7},{6,4},{7,5},{8,10},{9,11},{10,... | collective-permute-start | bytes 393224 | tf_op jit(solution)/shard_map/ppermute | solution.py:28
  18.1 6.9 %collective-permute-start.6 = (bf16[128,512]{1,0:T(8,128)(2,1)S(1)}, bf16[128,512]{1,0:T(8,128)(2,1)S(1)}, u32[]{:S(2)}, u32[]{:S(2)}) collective-permute-start(bf16[128,512]{1,0:T(8,128)(2,1)S(1)} %get-tuple-element.51), channel_id=1, source_target_pairs={{0,2},{1,3},{2,0},{3,1},{4,6},{5,7},{6,4},{7,5},{8,10},{9,11},{10,... | collective-permute-start | bytes 393224 | tf_op jit(solution)/shard_map/ppermute | solution.py:28
  19.2 6.0 %collective-permute-start.3 = (bf16[128,512]{1,0:T(8,128)(2,1)S(1)}, bf16[128,512]{1,0:T(8,128)(2,1)S(1)}, u32[]{:S(2)}, u32[]{:S(2)}) collective-permute-start(bf16[128,512]{1,0:T(8,128)(2,1)S(1)} %get-tuple-element.48), channel_id=1, source_target_pairs={{0,1},{1,0},{2,3},{3,2},{4,5},{5,4},{6,7},{7,6},{8,9},{9,8},{10,11... | collective-permute-start | bytes 393224 | tf_op jit(solution)/shard_map/ppermute | solution.py:28
  19.8 6.9 %collective-permute-start.5 = (bf16[128,512]{1,0:T(8,128)(2,1)S(1)}, bf16[128,512]{1,0:T(8,128)(2,1)S(1)}, u32[]{:S(2)}, u32[]{:S(2)}) collective-permute-start(bf16[128,512]{1,0:T(8,128)(2,1)S(1)} %add_convert_fusion.7), channel_id=1, source_target_pairs={{0,2},{1,3},{2,0},{3,1},{4,6},{5,7},{6,4},{7,5},{8,10},{9,11},{10,... | collective-permute-start | bytes 393224 | tf_op jit(solution)/shard_map/ppermute | solution.py:28
  30.6 5.5 %collective-permute-start.10 = (bf16[128,256]{1,0:T(8,128)(2,1)S(1)}, bf16[128,256]{1,0:T(8,128)(2,1)S(1)}, u32[]{:S(2)}, u32[]{:S(2)}) collective-permute-start(bf16[128,256]{1,0:T(8,128)(2,1)S(1)} %add_convert_fusion.19), channel_id=1, source_target_pairs={{0,8},{4,12},{8,0},{12,4},{16,24},{20,28},{24,16},{28,20},{1,9},{5... | collective-permute-start | bytes 196616 | tf_op jit(solution)/shard_map/ppermute | solution.py:28
  33.5 5.6 %collective-permute-start.16 = (bf16[128,256]{1,0:T(8,128)(2,1)S(1)}, bf16[128,256]{1,0:T(8,128)(2,1)S(1)}, u32[]{:S(2)}, u32[]{:S(2)}) collective-permute-start(bf16[128,256]{1,0:T(8,128)(2,1)S(1)} %add_convert_fusion.15), channel_id=1, source_target_pairs={{0,16},{4,20},{8,24},{12,28},{16,0},{20,4},{24,8},{28,12},{1,17},{... | collective-permute-start | bytes 196616 | tf_op jit(solution)/shard_map/ppermute | solution.py:28
  36.2 5.5 %collective-permute-start.11 = (bf16[128,256]{1,0:T(8,128)(2,1)S(1)}, bf16[128,256]{1,0:T(8,128)(2,1)S(1)}, u32[]{:S(2)}, u32[]{:S(2)}) collective-permute-start(bf16[128,256]{1,0:T(8,128)(2,1)S(1)} %add_convert_fusion.18), channel_id=1, source_target_pairs={{0,16},{4,20},{8,24},{12,28},{16,0},{20,4},{24,8},{28,12},{1,17},{... | collective-permute-start | bytes 196616 | tf_op jit(solution)/shard_map/ppermute | solution.py:28
  48.2 6.0 %collective-permute-start.23 = (bf16[128,512]{1,0:T(8,128)(2,1)S(1)}, bf16[128,512]{1,0:T(8,128)(2,1)S(1)}, u32[]{:S(2)}, u32[]{:S(2)}) collective-permute-start(bf16[128,512]{1,0:T(8,128)(2,1)S(1)} %shard_map.117), channel_id=1, source_target_pairs={{0,1},{1,0},{2,3},{3,2},{4,5},{5,4},{6,7},{7,6},{8,9},{9,8},{10,11... | collective-permute-start | bytes 393224 | tf_op jit(solution)/shard_map/ppermute | solution.py:28
  49.2 6.8 %collective-permute-start.21 = (bf16[128,512]{1,0:T(8,128)(2,1)S(1)}, bf16[128,512]{1,0:T(8,128)(2,1)S(1)}, u32[]{:S(2)}, u32[]{:S(2)}) collective-permute-start(bf16[128,512]{1,0:T(8,128)(2,1)S(1)} %shard_map.116), channel_id=1, source_target_pairs={{0,2},{1,3},{2,0},{3,1},{4,6},{5,7},{6,4},{7,5},{8,10},{9,11},{10,... | collective-permute-start | bytes 393224 | tf_op jit(solution)/shard_map/ppermute | solution.py:28
  64.9 6.5 %collective-permute-start.30 = (bf16[128,256]{1,0:T(8,128)(2,1)S(1)}, bf16[128,256]{1,0:T(8,128)(2,1)S(1)}, u32[]{:S(2)}, u32[]{:S(2)}) collective-permute-start(bf16[128,256]{1,0:T(8,128)(2,1)S(1)} %add_convert_fusion.10), channel_id=1, source_target_pairs={{0,8},{4,12},{8,0},{12,4},{16,24},{20,28},{24,16},{28,20},{1,9},{5... | collective-permute-start | bytes 196616 | tf_op jit(solution)/shard_map/ppermute | solution.py:28
  67.4 8.2 %collective-permute-start.27 = (bf16[128,256]{1,0:T(8,128)(2,1)S(1)}, bf16[128,256]{1,0:T(8,128)(2,1)S(1)}, u32[]{:S(2)}, u32[]{:S(2)}) collective-permute-start(bf16[128,256]{1,0:T(8,128)(2,1)S(1)} %add_convert_fusion.12), channel_id=1, source_target_pairs={{0,16},{4,20},{8,24},{12,28},{16,0},{20,4},{24,8},{28,12},{1,17},{... | collective-permute-start | bytes 196616 | tf_op jit(solution)/shard_map/ppermute | solution.py:28
  71.4 5.8 %collective-permute-start.31 = (bf16[128,256]{1,0:T(8,128)(2,1)S(1)}, bf16[128,256]{1,0:T(8,128)(2,1)S(1)}, u32[]{:S(2)}, u32[]{:S(2)}) collective-permute-start(bf16[128,256]{1,0:T(8,128)(2,1)S(1)} %add_convert_fusion.9), channel_id=1, source_target_pairs={{0,16},{4,20},{8,24},{12,28},{16,0},{20,4},{24,8},{28,12},{1,17},{... | collective-permute-start | bytes 196616 | tf_op jit(solution)/shard_map/ppermute | solution.py:28
  83.0 6.4 %collective-permute-start.38 = (bf16[128,512]{1,0:T(8,128)(2,1)S(1)}, bf16[128,512]{1,0:T(8,128)(2,1)S(1)}, u32[]{:S(2)}, u32[]{:S(2)}) collective-permute-start(bf16[128,512]{1,0:T(8,128)(2,1)S(1)} %get-tuple-element.72.refs_0_), channel_id=1, source_target_pairs={{0,2},{1,3},{2,0},{3,1},{4,6},{5,7},{6,4},{7,5},{8,10},{9,11},{10,... | collective-permute-start | bytes 393224 | tf_op jit(solution)/shard_map/ppermute | solution.py:28
  83.9 6.4 %collective-permute-start.37 = (bf16[128,512]{1,0:T(8,128)(2,1)S(1)}, bf16[128,512]{1,0:T(8,128)(2,1)S(1)}, u32[]{:S(2)}, u32[]{:S(2)}) collective-permute-start(bf16[128,512]{1,0:T(8,128)(2,1)S(1)} %get-tuple-element.73.refs_1_), channel_id=1, source_target_pairs={{0,1},{1,0},{2,3},{3,2},{4,5},{5,4},{6,7},{7,6},{8,9},{9,8},{10,11... | collective-permute-start | bytes 393224 | tf_op jit(solution)/shard_map/ppermute | solution.py:28
  85.0 8.0 %collective-permute-start.39 = (bf16[128,512]{1,0:T(8,128)(2,1)S(1)}, bf16[128,512]{1,0:T(8,128)(2,1)S(1)}, u32[]{:S(2)}, u32[]{:S(2)}) collective-permute-start(bf16[128,512]{1,0:T(8,128)(2,1)S(1)} %get-tuple-element.72.refs_0_), channel_id=1, source_target_pairs={{0,1},{1,0},{2,3},{3,2},{4,5},{5,4},{6,7},{7,6},{8,9},{9,8},{10,11... | collective-permute-start | bytes 393224 | tf_op jit(solution)/shard_map/ppermute | solution.py:28
  85.9 7.2 %collective-permute-start.40 = (bf16[128,512]{1,0:T(8,128)(2,1)S(1)}, bf16[128,512]{1,0:T(8,128)(2,1)S(1)}, u32[]{:S(2)}, u32[]{:S(2)}) collective-permute-start(bf16[128,512]{1,0:T(8,128)(2,1)S(1)} %get-tuple-element.73.refs_1_), channel_id=1, source_target_pairs={{0,2},{1,3},{2,0},{3,1},{4,6},{5,7},{6,4},{7,5},{8,10},{9,11},{10,... | collective-permute-start | bytes 393224 | tf_op jit(solution)/shard_map/ppermute | solution.py:28
  96.0 5.5 %collective-permute-start.47 = (bf16[128,512]{1,0:T(8,128)(2,1)S(1)}, bf16[128,512]{1,0:T(8,128)(2,1)S(1)}, u32[]{:S(2)}, u32[]{:S(2)}) collective-permute-start(bf16[128,512]{1,0:T(8,128)(2,1)S(1)} %get-tuple-element.82), channel_id=1, source_target_pairs={{0,2},{1,3},{2,0},{3,1},{4,6},{5,7},{6,4},{7,5},{8,10},{9,11},{10,... | collective-permute-start | bytes 393224 | tf_op jit(solution)/shard_map/ppermute | solution.py:28
  97.3 6.4 %collective-permute-start.44 = (bf16[128,512]{1,0:T(8,128)(2,1)S(1)}, bf16[128,512]{1,0:T(8,128)(2,1)S(1)}, u32[]{:S(2)}, u32[]{:S(2)}) collective-permute-start(bf16[128,512]{1,0:T(8,128)(2,1)S(1)} %get-tuple-element.78), channel_id=1, source_target_pairs={{0,1},{1,0},{2,3},{3,2},{4,5},{5,4},{6,7},{7,6},{8,9},{9,8},{10,11... | collective-permute-start | bytes 393224 | tf_op jit(solution)/shard_map/ppermute | solution.py:28
  97.9 7.1 %collective-permute-start.46 = (bf16[128,512]{1,0:T(8,128)(2,1)S(1)}, bf16[128,512]{1,0:T(8,128)(2,1)S(1)}, u32[]{:S(2)}, u32[]{:S(2)}) collective-permute-start(bf16[128,512]{1,0:T(8,128)(2,1)S(1)} %get-tuple-element.80), channel_id=1, source_target_pairs={{0,2},{1,3},{2,0},{3,1},{4,6},{5,7},{6,4},{7,5},{8,10},{9,11},{10,... | collective-permute-start | bytes 393224 | tf_op jit(solution)/shard_map/ppermute | solution.py:28
  99.5 8.1 %collective-permute-start.43 = (bf16[128,512]{1,0:T(8,128)(2,1)S(1)}, bf16[128,512]{1,0:T(8,128)(2,1)S(1)}, u32[]{:S(2)}, u32[]{:S(2)}) collective-permute-start(bf16[128,512]{1,0:T(8,128)(2,1)S(1)} %get-tuple-element.76), channel_id=1, source_target_pairs={{0,1},{1,0},{2,3},{3,2},{4,5},{5,4},{6,7},{7,6},{8,9},{9,8},{10,11... | collective-permute-start | bytes 393224 | tf_op jit(solution)/shard_map/ppermute | solution.py:28
  101.5 5.3 %collective-permute-start.48 = (bf16[128,512]{1,0:T(8,128)(2,1)S(1)}, bf16[128,512]{1,0:T(8,128)(2,1)S(1)}, u32[]{:S(2)}, u32[]{:S(2)}) collective-permute-start(bf16[128,512]{1,0:T(8,128)(2,1)S(1)} %add_convert_fusion), channel_id=1, source_target_pairs={{0,1},{1,0},{2,3},{3,2},{4,5},{5,4},{6,7},{7,6},{8,9},{9,8},{10,11... | collective-permute-start | bytes 393224 | tf_op jit(solution)/shard_map/ppermute | solution.py:28
  (28 other events, 127.0 us)
where the time goes:
time: 110 us
  starting transfers between devices  48.7 us (44%)
  waiting for transfers between devices  45.2 us (41%)
  Pallas kernels  14.5 us (13%)
    ppermute x49, starting transfers between devices, exchange(): lax.ppermute(values, axis, [(i, partner(i, step, size)) for i in range(si...  48.7 us
    ppermute x49, waiting for transfers between devices, exchange(): lax.ppermute(values, axis, [(i, partner(i, step, size)) for i in range(si...  45.2 us
    pallas_call x28, Pallas kernels, call(): pl.pallas_call(kernel, in_specs=in_specs, out_specs=[smem if dtype == jnp...  14.5 us
  transfers between devices with their start and end apart: 49, of which 30 were waited for; matrix products, arithmetic and copies ran while one was open for 0% of the time, Pallas kernels for 7%

commit v1 on v0

--- a/solution.py
+++ b/solution.py
@@ -14,6 +14,7 @@
 SHARE_FLOPS = 2 * 10**8
 F32 = jnp.float32
 BF16 = jnp.bfloat16
+GROUP, MEMBER = "group", "member"
 
 
 def is_power_of_two(size):
@@ -122,7 +123,7 @@
     terms = refs[: len(which)]
     before = refs[len(which) : -1]
     pivot_blocks = inverse_ref.shape[2] // BLOCK
-    member = lax.axis_index("member")
+    member = lax.axis_index(MEMBER)
     total = before[0][...] if before else None
     for k, term in zip(which, terms):
         owner = traced_source(member, k, members)
@@ -141,11 +142,10 @@
     forward_ref[...] = total.astype(forward_ref.dtype)
 
 
-def mid_piece_kernel(members, step, border_ref, forward_ref, low_ref, high_ref):
-    owner = traced_partner(lax.axis_index("member"), step, members)
-    rows = low_ref.shape[1]
-    for half, ref in enumerate((low_ref, high_ref)):
-        piece = border_piece(border_ref, 2 * owner + half, rows)
+def mid_piece_kernel(members, step, halves, border_ref, forward_ref, *outs):
+    owner = traced_partner(lax.axis_index(MEMBER), step, members)
+    for half, ref in zip(halves, outs):
+        piece = border_piece(border_ref, 2 * owner + half, ref.shape[1])
         ref[...] = (-times_transpose(forward_ref[...], piece)).astype(BF16)
 
 
@@ -153,7 +153,7 @@
     map_ref, border_ref, forward_ref = refs[:3]
     terms = refs[3 : 3 + members]
     update_ref = refs[-1]
-    member = lax.axis_index("member")
+    member = lax.axis_index(MEMBER)
     rows = update_ref.shape[1]
     piece = border_ref[0, pl.ds(pl.multiple_of(member * rows, BLOCK), rows), :]
     update_ref[...] = -times_transpose(forward_ref[...], piece)
@@ -178,7 +178,7 @@
 def stream_places(core, chips, share):
     if not is_split(chips):
         return [[core * (share // 2)]], share // 2
-    chip = lax.axis_index("group") // 2
+    chip = lax.axis_index(GROUP) // 2
     size = share // (4 * chips)
     owners = [2 * lax.bitwise_xor(chip, jnp.int32(k)) + core for k in DISTANCES]
     return [[(2 * owner + stream) * size for owner in owners] for stream in range(2)], size
@@ -208,7 +208,7 @@
     inputs, outs, spread = refs[: -1 - 2 * count], refs[-1 - 2 * count : -1], refs[-1]
     map_ref, own_ref = inputs[:2]
     arrived = (inputs[2 : 2 + lows], inputs[2 + lows :])
-    core = lax.axis_index("group") & 1
+    core = lax.axis_index(GROUP) & 1
     spread[...] = jnp.zeros_like(spread)
     half_blocks = own_ref.shape[1] // (2 * BLOCK)
     for i in range(2 * half_blocks):
@@ -221,7 +221,7 @@
 
 
 def join(joined, units, chips):
-    core = lax.axis_index("group") & 1
+    core = lax.axis_index(GROUP) & 1
     count = len(units) // 2
     for owner, refs in ((core, units[:count]), (1 - core, units[count:])):
         places_of, size = unit_places(owner, chips, joined.shape[1])
@@ -232,7 +232,7 @@
 
 
 def root_product(chips, which, units, inverse_ref, lines):
-    core = lax.axis_index("group") & 1
+    core = lax.axis_index(GROUP) & 1
     total = None
     for (own, number), ref in zip(which, units):
         places_of, size = unit_places(core if own else 1 - core, chips, inverse_ref.shape[1])
@@ -257,18 +257,14 @@
     out_ref[...] = (total + before_ref[...]).astype(BF16)
 
 
-def root_back_kernel(chips, owners, part, inverse_ref, forward_ref, *refs):
-    count = len(owners) * (2 if is_split(chips) else 1)
-    before, outs = refs[:-count], refs[-count:]
-    core = lax.axis_index("group") & 1
-    places_of = []
-    for own in owners:
-        streams, size = stream_places(core if own else 1 - core, chips, inverse_ref.shape[1])
-        places_of += streams
+def root_back_kernel(chips, which, part, inverse_ref, forward_ref, *refs):
+    before, outs = refs[: -len(which)], refs[-len(which) :]
+    core = lax.axis_index(GROUP) & 1
     forward = forward_ref[...]
     lines = pl.ds(part * forward.shape[1], forward.shape[1])
-    for i, (places, out_ref) in enumerate(zip(places_of, outs)):
-        total = times(forward, at_places(inverse_ref, lines, places, size))
+    for i, ((own, number), out_ref) in enumerate(zip(which, outs)):
+        streams, size = stream_places(core if own else 1 - core, chips, inverse_ref.shape[1])
+        total = times(forward, at_places(inverse_ref, lines, streams[number], size))
         if before:
             total = total + before[i][...]
         out_ref[...] = total.astype(out_ref.dtype)
@@ -292,7 +288,7 @@
 def root_slice_kernel(mine_ref, other_ref, out_ref, joined, turned):
     join(joined, (mine_ref, other_ref), 1)
     rows_out = out_ref.shape[1]
-    first = lax.axis_index("group") * rows_out
+    first = lax.axis_index(GROUP) * rows_out
     rows = turned.shape[0]
     turned[...] = joined[:, at_part(first // rows, rows)].astype(F32).T
     begin = pl.multiple_of(lax.rem(first, jnp.int32(rows)), min(rows_out, rows))
@@ -300,7 +296,7 @@
 
 
 def border_product(members, values, which, border_ref):
-    member = lax.axis_index("member")
+    member = lax.axis_index(MEMBER)
     total = None
     for (step, half), ref in zip(which, values):
         owner = traced_source(member, step, members)
@@ -330,13 +326,13 @@
     part_ref, asked_ref, piece_ref = refs[-3:]
     back = back_ref[...] - border_product(members, values, late, border_ref)
     part_ref[...] = times(back.astype(BF16), inverse_ref[0]).astype(BF16)
-    owner = traced_partner(lax.axis_index("member"), members - 1, members)
+    owner = traced_partner(lax.axis_index(MEMBER), members - 1, members)
     ask(map_ref, owner, part_ref, asked_ref)
     piece_ref[...] = part_ref[:, at_part(owner, piece_ref.shape[1])]
 
 
 def mid_share_kernel(members, step, map_ref, part_ref, asked_ref, piece_ref):
-    owner = traced_partner(lax.axis_index("member"), step, members)
+    owner = traced_partner(lax.axis_index(MEMBER), step, members)
     ask(map_ref, owner, part_ref, asked_ref)
     piece_ref[...] = part_ref[:, at_part(owner, piece_ref.shape[1])]
 
@@ -344,7 +340,7 @@
 def pick_kernel(members, map_ref, part_ref, *refs):
     values = refs[:-2]
     base_ref, own_ref = refs[-2:]
-    member = lax.axis_index("member")
+    member = lax.axis_index(MEMBER)
     pivot_blocks = part_ref.shape[1] // BLOCK
     rows = values[0].shape[1]
     for j in range(base_ref.shape[1] // BLOCK):
@@ -431,32 +427,32 @@
 
 def group_sum(mine, other, size, chips):
     if not is_split(chips):
-        total = total_of(mine[0], [exchange(other[0], "group", 1, size)])
-        total = total_of(total, [exchange(total, "group", k, size) for k in range(2, size, 2)])
-        return [total], [exchange(total, "group", 1, size)]
+        total = total_of(mine[0], [exchange(other[0], GROUP, 1, size)])
+        total = total_of(total, [exchange(total, GROUP, k, size) for k in range(2, size, 2)])
+        return [total], [exchange(total, GROUP, 1, size)]
     own_units, other_units = [], []
     for kept, given in zip(mine, other):
         rows = kept.shape[1] // 2
         block = rows // 2
         low, high = split(kept, rows)
-        low_core, high_core = split(exchange(given, "group", 1, size), rows)
-        pair = exchange(total_of(high, [high_core]), "group", 2, size)
+        low_core, high_core = split(exchange(given, GROUP, 1, size), rows)
+        pair = exchange(total_of(high, [high_core]), GROUP, 2, size)
         side = total_of(low, [low_core, pair])
-        far, near = split(exchange(side, "group", 4, size), block)
+        far, near = split(exchange(side, GROUP, 4, size), block)
         unit = total_of(side, [jnp.concatenate([near, far], axis=1)])
-        rest = exchange(unit, "group", 2, size)
+        rest = exchange(unit, GROUP, 2, size)
         own_units += [unit, rest]
-        other_units += [exchange(unit, "group", 1, size), exchange(rest, "group", 1, size)]
+        other_units += [exchange(unit, GROUP, 1, size), exchange(rest, GROUP, 1, size)]
     return own_units, other_units
 
 
 def member_sum(low, high, size):
     if not is_power_of_two(size):
-        return lax.psum(low, "member"), lax.psum(high, "member")
+        return lax.psum(low, MEMBER), lax.psum(high, MEMBER)
     steps = [1 << i for i in range(size.bit_length() - 1)]
     for first, second in zip(steps, reversed(steps)):
-        other_low = exchange(low, "member", first, size)
-        other_high = exchange(high, "member", second, size)
+        other_low = exchange(low, MEMBER, first, size)
+        other_high = exchange(high, MEMBER, second, size)
         low, high = total_of(low, [other_low]), total_of(high, [other_high])
     return low, high
 
@@ -469,17 +465,17 @@
     rows = pieces[0][0].shape[1]
     if size != 4:
         arrived = [
-            split(exchange(jnp.concatenate(pair, axis=1), "member", k, size), rows)
+            split(exchange(jnp.concatenate(pair, axis=1), MEMBER, k, size), rows)
             for k, pair in enumerate(pieces, start=1)
         ]
         return [low for low, _ in arrived], [high for _, high in arrived]
     (low1, high1), (low2, high2), (low3, high3) = pieces
-    relay1 = exchange(low3, "member", 1, size)
-    relay2 = exchange(high3, "member", 2, size)
-    first1 = exchange(low1, "member", 1, size)
-    first2 = exchange(high2, "member", 2, size)
-    last2 = exchange(total_of(low2, [relay1]), "member", 2, size)
-    last1 = exchange(total_of(high1, [relay2]), "member", 1, size)
+    relay1 = exchange(low3, MEMBER, 1, size)
+    relay2 = exchange(high3, MEMBER, 2, size)
+    first1 = exchange(low1, MEMBER, 1, size)
+    first2 = exchange(high2, MEMBER, 2, size)
+    last2 = exchange(total_of(low2, [relay1]), MEMBER, 2, size)
+    last1 = exchange(total_of(high1, [relay2]), MEMBER, 1, size)
     return [first1, last2], [first2, last1]
 
 
@@ -488,14 +484,14 @@
     if size != 4:
         values = jnp.concatenate([low, high], axis=1)
         return [(low, high)] + [
-            split(exchange(values, "member", k, size), rows) for k in range(1, size)
+            split(exchange(values, MEMBER, k, size), rows) for k in range(1, size)
         ]
-    high1 = exchange(high, "member", 1, size)
-    low2 = exchange(low, "member", 2, size)
-    low1 = exchange(low, "member", 1, size)
-    high2 = exchange(high, "member", 2, size)
-    low3 = exchange(low2, "member", 1, size)
-    high3 = exchange(high1, "member", 2, size)
+    high1 = exchange(high, MEMBER, 1, size)
+    low2 = exchange(low, MEMBER, 2, size)
+    low1 = exchange(low, MEMBER, 1, size)
+    high2 = exchange(high, MEMBER, 2, size)
+    low3 = exchange(low2, MEMBER, 1, size)
+    high3 = exchange(high1, MEMBER, 2, size)
     return [(low, high), (low1, high1), (low2, high2), (low3, high3)]
 
 
@@ -526,7 +522,7 @@
             return ((columns, rows), dtype)
 
         def spread_over_members(values):
-            return [values] + [exchange(values, "member", k, members) for k in steps]
+            return [values] + [exchange(values, MEMBER, k, members) for k in steps]
 
         leaf_forward, leaf_factor, leaf_edge, leaf_map, root_map = call(
             leaf_forward_kernel,
@@ -563,15 +559,17 @@
             )
         (mid_forward,) = mid_forward
         half_border = own_border // 2
-        pieces = {
-            k: call(
-                functools.partial(mid_piece_kernel, members, k),
-                [mid_border, mid_forward],
-                [flat(half_border), flat(half_border)],
-                flops=2 * columns * own_pivots * own_border,
-            )
-            for k in reversed(steps)
-        }
+        pieces = {k: () for k in steps}
+        for k in reversed(steps):
+            for halves in [(0,), (1,)] if k == members - 1 else [(0, 1)]:
+                pieces[k] += tuple(
+                    call(
+                        functools.partial(mid_piece_kernel, members, k, halves),
+                        [mid_border, mid_forward],
+                        [flat(half_border)] * len(halves),
+                        flops=columns * own_pivots * own_border * len(halves),
+                    )
+                )
         lows, highs = scatter_sum([pieces[k] for k in steps], members)
         (own_update,) = call(
             functools.partial(own_update_kernel, members, pivots // BLOCK),
@@ -619,21 +617,22 @@
             for part, total in enumerate(before)
         ]
         root_forward = member_sum(*root_parts, members)
+        streams = [(own, number) for own in (0, 1) for number in range(count)]
         first = call(
-            functools.partial(root_back_kernel, chips, (0, 1), 0),
+            functools.partial(root_back_kernel, chips, streams, 0),
             [root_inverse, root_forward[0]],
             [(shape, F32) for shape, _ in half_streams * 2],
             flops=root_flops,
         )
-        other, mine = (
-            call(
-                functools.partial(root_back_kernel, chips, (own,), 1),
-                [root_inverse, root_forward[1], *first[own * count : (own + 1) * count]],
-                half_streams,
-                flops=root_flops // 2,
+        halves = []
+        for begin, end in [(i, i + 1) for i in range(count)] + [(count, 2 * count)]:
+            halves += call(
+                functools.partial(root_back_kernel, chips, streams[begin:end], 1),
+                [root_inverse, root_forward[1], *first[begin:end]],
+                half_streams[: end - begin],
+                flops=root_flops * (end - begin) // (2 * count),
             )
-            for own in (0, 1)
-        )
+        other, mine = halves[:count], halves[count:]
         mine, other = group_sum(mine, other, groups, chips)
         own_values = call(
             functools.partial(root_pick_kernel, chips),
@@ -696,21 +695,21 @@
 
 def solution(mesh):
     in_specs = (
-        P("group", "member", None, None),
-        P("group", "member", None, None),
-        P("group", "member", None, None),
-        P("group", None, None),
-        P("group", "member", None),
-        P("group", None, "member"),
-        P("group", "member", None),
-        P("group", "member"),
+        P(GROUP, MEMBER, None, None),
+        P(GROUP, MEMBER, None, None),
+        P(GROUP, MEMBER, None, None),
+        P(GROUP, None, None),
+        P(GROUP, MEMBER, None),
+        P(GROUP, None, MEMBER),
+        P(GROUP, MEMBER, None),
+        P(GROUP, MEMBER),
     )
     out_specs = (
-        P("group", "member", None, None),
-        P("group", "member", None),
-        P("member", "group", None),
+        P(GROUP, MEMBER, None, None),
+        P(GROUP, MEMBER, None),
+        P(MEMBER, GROUP, None),
     )
-    on_device = make_on_device(mesh.shape["group"], mesh.shape["member"])
+    on_device = make_on_device(mesh.shape[GROUP], mesh.shape[MEMBER])
 
     return jax.shard_map(
         on_device, mesh=mesh, in_specs=in_specs, out_specs=out_specs, check_vma=False

time: 110 us -> 110 us (level)
    pallas_call x28 -> x30, Pallas kernels: 14.5 us -> 14.8 us  [call(): pl.pallas_call(kernel, in_specs=in_specs, out_specs=[smem if dtype == jnp...]
  transfers between devices with their start and end apart: 49 -> 49, of which waited for: 30 -> 29; matrix products, arithmetic and copies ran while one was open for 0% -> 0% of each run, Pallas kernels for 7% -> 8%
where the time goes in v1:
time: 110 us
  starting transfers between devices  48.7 us (44%)
  waiting for transfers between devices  44.9 us (41%)
  Pallas kernels  14.8 us (13%)
    ppermute x49, starting transfers between devices, exchange(): lax.ppermute(values, axis, [(i, partner(i, step, size)) for i in range(si...  48.7 us
    ppermute x49, waiting for transfers between devices, exchange(): lax.ppermute(values, axis, [(i, partner(i, step, size)) for i in range(si...  44.9 us
    pallas_call x30, Pallas kernels, call(): pl.pallas_call(kernel, in_specs=in_specs, out_specs=[smem if dtype == jnp...  14.8 us
  transfers between devices with their start and end apart: 49, of which 29 were waited for; matrix products, arithmetic and copies ran while one was open for 0% of the time, Pallas kernels for 8%

profile of v1, /device:TPU:0, one launch (start us, length us, event | category | flops | bytes accessed | tf_op | source)
XLA Modules:
  0.0 110.0 jit_solution(14809630301504181320)
XLA Ops:
  0.6 2.0 %shard_map.103 = (bf16[128,768]{1,0:T(8,128)(2,1)S(1)}, bf16[768,768]{1,0:T(8,128)(2,1)S(1)}, bf16[512,768]{1,0:T(8,128)(2,1)S(1)}, s32[1,4,4]{2,1,0:T(4,128)S(4)}, s32[1,1,8]{2,1,0:T(1,128)S(4)}) custom-call(bf16[1,1,768,128]{3,2,1,0:T(8,128)(2,1)} %rhs_hbm.1, bf16[1,1,768,768]{3,2,1,0:T(8,128)(2,1)} %factor_hbm.1, bf16[1,1,512,768]{3,2,1,0:T(8,128)(2,1)} %edge_hbm.1, ...), custom_call_target="tpu_custom_call" | custom-call | flops 150994944 | bytes 2162784 | tf_op jit(solution)/shard_map/pallas_call | solution.py:405
  3.0 4.0 %collective-permute-start.2 = (bf16[128,512]{1,0:T(8,128)(2,1)S(1)}, bf16[128,512]{1,0:T(8,128)(2,1)S(1)}, u32[]{:S(2)}, u32[]{:S(2)}) collective-permute-start(bf16[128,512]{1,0:T(8,128)(2,1)S(1)} %shard_map.104.refs_0_.refs_3_), channel_id=1, source_target_pairs={{0,3},{1,2},{2,1},{3,0},{4,7},{5,6},{6,5},{7,4},{8,11},{9,10},{10,... | collective-permute-start | bytes 393224 | tf_op jit(solution)/shard_map/ppermute | solution.py:29
  8.0 3.4 %collective-permute-done.2.refs_0_.refs_6_ = bf16[128,512]{1,0:T(8,128)(2,1)S(1)} collective-permute-done((bf16[128,512]{1,0:T(8,128)(2,1)S(1)}, bf16[128,512]{1,0:T(8,128)(2,1)S(1)}, u32[]{:S(2)}, u32[]{:S(2)}) %collective-permute-start.2) | collective-permute-done | bytes 131104 | tf_op jit(solution)/shard_map/ppermute | solution.py:29
  11.7 1.9 %collective-permute-done.1.refs_1_.refs_4_ = bf16[128,512]{1,0:T(8,128)(2,1)S(1)} collective-permute-done((bf16[128,512]{1,0:T(8,128)(2,1)S(1)}, bf16[128,512]{1,0:T(8,128)(2,1)S(1)}, u32[]{:S(2)}, u32[]{:S(2)}) %collective-permute-start.1) | collective-permute-done | bytes 131104 | tf_op jit(solution)/shard_map/ppermute | solution.py:29
  14.4 1.6 %collective-permute-start.4 = (bf16[128,512]{1,0:T(8,128)(2,1)S(1)}, bf16[128,512]{1,0:T(8,128)(2,1)S(1)}, u32[]{:S(2)}, u32[]{:S(2)}) collective-permute-start(bf16[128,512]{1,0:T(8,128)(2,1)S(1)} %shard_map.111), channel_id=1, source_target_pairs={{0,1},{1,0},{2,3},{3,2},{4,5},{5,4},{6,7},{7,6},{8,9},{9,8},{10,11... | collective-permute-start | bytes 393224 | tf_op jit(solution)/shard_map/ppermute | solution.py:29
  29.2 1.6 %collective-permute-start.15 = (bf16[128,256]{1,0:T(8,128)(2,1)S(1)}, bf16[128,256]{1,0:T(8,128)(2,1)S(1)}, u32[]{:S(2)}, u32[]{:S(2)}) collective-permute-start(bf16[128,256]{1,0:T(8,128)(2,1)S(1)} %add_convert_fusion.16), channel_id=1, source_target_pairs={{0,8},{4,12},{8,0},{12,4},{16,24},{20,28},{24,16},{28,20},{1,9},{5... | collective-permute-start | bytes 196616 | tf_op jit(solution)/shard_map/ppermute | solution.py:29
  31.4 2.3 %collective-permute-done.15 = bf16[128,256]{1,0:T(8,128)(2,1)S(1)} collective-permute-done((bf16[128,256]{1,0:T(8,128)(2,1)S(1)}, bf16[128,256]{1,0:T(8,128)(2,1)S(1)}, u32[]{:S(2)}, u32[]{:S(2)}) %collective-permute-start.15) | collective-permute-done | bytes 65568 | tf_op jit(solution)/shard_map/ppermute | solution.py:29
  33.7 2.7 %collective-permute-start.16 = (bf16[128,256]{1,0:T(8,128)(2,1)S(1)}, bf16[128,256]{1,0:T(8,128)(2,1)S(1)}, u32[]{:S(2)}, u32[]{:S(2)}) collective-permute-start(bf16[128,256]{1,0:T(8,128)(2,1)S(1)} %add_convert_fusion.15), channel_id=1, source_target_pairs={{0,16},{4,20},{8,24},{12,28},{16,0},{20,4},{24,8},{28,12},{1,17},{... | collective-permute-start | bytes 196616 | tf_op jit(solution)/shard_map/ppermute | solution.py:29
  36.4 1.5 %collective-permute-start.11 = (bf16[128,256]{1,0:T(8,128)(2,1)S(1)}, bf16[128,256]{1,0:T(8,128)(2,1)S(1)}, u32[]{:S(2)}, u32[]{:S(2)}) collective-permute-start(bf16[128,256]{1,0:T(8,128)(2,1)S(1)} %add_convert_fusion.18), channel_id=1, source_target_pairs={{0,16},{4,20},{8,24},{12,28},{16,0},{20,4},{24,8},{28,12},{1,17},{... | collective-permute-start | bytes 196616 | tf_op jit(solution)/shard_map/ppermute | solution.py:29
  39.3 2.6 %collective-permute-start.17 = (bf16[128,256]{1,0:T(8,128)(2,1)S(1)}, bf16[128,256]{1,0:T(8,128)(2,1)S(1)}, u32[]{:S(2)}, u32[]{:S(2)}) collective-permute-start(bf16[128,256]{1,0:T(8,128)(2,1)S(1)} %add_convert_fusion.14.refs_0_), channel_id=1, source_target_pairs={{0,8},{4,12},{8,0},{12,4},{16,24},{20,28},{24,16},{28,20},{1,9},{5... | collective-permute-start | bytes 196616 | tf_op jit(solution)/shard_map/ppermute | solution.py:29
  42.0 1.8 %collective-permute-start.12 = (bf16[128,256]{1,0:T(8,128)(2,1)S(1)}, bf16[128,256]{1,0:T(8,128)(2,1)S(1)}, u32[]{:S(2)}, u32[]{:S(2)}) collective-permute-start(bf16[128,256]{1,0:T(8,128)(2,1)S(1)} %add_convert_fusion.17.refs_1_), channel_id=1, source_target_pairs={{0,8},{4,12},{8,0},{12,4},{16,24},{20,28},{24,16},{28,20},{1,9},{5... | collective-permute-start | bytes 196616 | tf_op jit(solution)/shard_map/ppermute | solution.py:29
  44.4 2.0 %collective-permute-done.12.refs_0_ = bf16[128,256]{1,0:T(8,128)(2,1)S(1)} collective-permute-done((bf16[128,256]{1,0:T(8,128)(2,1)S(1)}, bf16[128,256]{1,0:T(8,128)(2,1)S(1)}, u32[]{:S(2)}, u32[]{:S(2)}) %collective-permute-start.12) | collective-permute-done | bytes 65568 | tf_op jit(solution)/shard_map/ppermute | solution.py:29
  49.3 1.7 %collective-permute-start.21 = (bf16[128,512]{1,0:T(8,128)(2,1)S(1)}, bf16[128,512]{1,0:T(8,128)(2,1)S(1)}, u32[]{:S(2)}, u32[]{:S(2)}) collective-permute-start(bf16[128,512]{1,0:T(8,128)(2,1)S(1)} %shard_map.117), channel_id=1, source_target_pairs={{0,2},{1,3},{2,0},{3,1},{4,6},{5,7},{6,4},{7,5},{8,10},{9,11},{10,... | collective-permute-start | bytes 393224 | tf_op jit(solution)/shard_map/ppermute | solution.py:29
  51.1 3.3 %collective-permute-done.23 = bf16[128,512]{1,0:T(8,128)(2,1)S(1)} collective-permute-done((bf16[128,512]{1,0:T(8,128)(2,1)S(1)}, bf16[128,512]{1,0:T(8,128)(2,1)S(1)}, u32[]{:S(2)}, u32[]{:S(2)}) %collective-permute-start.23) | collective-permute-done | bytes 131104 | tf_op jit(solution)/shard_map/ppermute | solution.py:29
  54.4 1.8 %collective-permute-start.24 = (bf16[128,512]{1,0:T(8,128)(2,1)S(1)}, bf16[128,512]{1,0:T(8,128)(2,1)S(1)}, u32[]{:S(2)}, u32[]{:S(2)}) collective-permute-start(bf16[128,512]{1,0:T(8,128)(2,1)S(1)} %add_convert_fusion.3), channel_id=1, source_target_pairs={{0,2},{1,3},{2,0},{3,1},{4,6},{5,7},{6,4},{7,5},{8,10},{9,11},{10,... | collective-permute-start | bytes 393224 | tf_op jit(solution)/shard_map/ppermute | solution.py:29
  56.9 2.6 %collective-permute-done.24 = bf16[128,512]{1,0:T(8,128)(2,1)S(1)} collective-permute-done((bf16[128,512]{1,0:T(8,128)(2,1)S(1)}, bf16[128,512]{1,0:T(8,128)(2,1)S(1)}, u32[]{:S(2)}, u32[]{:S(2)}) %collective-permute-start.24) | collective-permute-done | bytes 131104 | tf_op jit(solution)/shard_map/ppermute | solution.py:29
  63.1 1.9 %collective-permute-start.30 = (bf16[128,256]{1,0:T(8,128)(2,1)S(1)}, bf16[128,256]{1,0:T(8,128)(2,1)S(1)}, u32[]{:S(2)}, u32[]{:S(2)}) collective-permute-start(bf16[128,256]{1,0:T(8,128)(2,1)S(1)} %add_convert_fusion.10), channel_id=1, source_target_pairs={{0,8},{4,12},{8,0},{12,4},{16,24},{20,28},{24,16},{28,20},{1,9},{5... | collective-permute-start | bytes 196616 | tf_op jit(solution)/shard_map/ppermute | solution.py:29
  65.5 2.0 %collective-permute-done.30 = bf16[128,256]{1,0:T(8,128)(2,1)S(1)} collective-permute-done((bf16[128,256]{1,0:T(8,128)(2,1)S(1)}, bf16[128,256]{1,0:T(8,128)(2,1)S(1)}, u32[]{:S(2)}, u32[]{:S(2)}) %collective-permute-start.30) | collective-permute-done | bytes 65568 | tf_op jit(solution)/shard_map/ppermute | solution.py:29
  67.5 4.0 %collective-permute-start.31 = (bf16[128,256]{1,0:T(8,128)(2,1)S(1)}, bf16[128,256]{1,0:T(8,128)(2,1)S(1)}, u32[]{:S(2)}, u32[]{:S(2)}) collective-permute-start(bf16[128,256]{1,0:T(8,128)(2,1)S(1)} %add_convert_fusion.9), channel_id=1, source_target_pairs={{0,16},{4,20},{8,24},{12,28},{16,0},{20,4},{24,8},{28,12},{1,17},{... | collective-permute-start | bytes 196616 | tf_op jit(solution)/shard_map/ppermute | solution.py:29
  72.5 3.3 %collective-permute-done.31 = bf16[128,256]{1,0:T(8,128)(2,1)S(1)} collective-permute-done((bf16[128,256]{1,0:T(8,128)(2,1)S(1)}, bf16[128,256]{1,0:T(8,128)(2,1)S(1)}, u32[]{:S(2)}, u32[]{:S(2)}) %collective-permute-start.31) | collective-permute-done | bytes 65568 | tf_op jit(solution)/shard_map/ppermute | solution.py:29
  78.5 1.6 %collective-permute-done.32.refs_3_ = bf16[128,256]{1,0:T(8,128)(2,1)S(1)} collective-permute-done((bf16[128,256]{1,0:T(8,128)(2,1)S(1)}, bf16[128,256]{1,0:T(8,128)(2,1)S(1)}, u32[]{:S(2)}, u32[]{:S(2)}) %collective-permute-start.32) | collective-permute-done | bytes 65568 | tf_op jit(solution)/shard_map/ppermute | solution.py:29
  87.2 2.3 %collective-permute-done.38.refs_3_.refs_4_ = bf16[128,512]{1,0:T(8,128)(2,1)S(1)} collective-permute-done((bf16[128,512]{1,0:T(8,128)(2,1)S(1)}, bf16[128,512]{1,0:T(8,128)(2,1)S(1)}, u32[]{:S(2)}, u32[]{:S(2)}) %collective-permute-start.38) | collective-permute-done | bytes 131104 | tf_op jit(solution)/shard_map/ppermute | solution.py:29
  98.0 1.5 %collective-permute-start.46 = (bf16[128,512]{1,0:T(8,128)(2,1)S(1)}, bf16[128,512]{1,0:T(8,128)(2,1)S(1)}, u32[]{:S(2)}, u32[]{:S(2)}) collective-permute-start(bf16[128,512]{1,0:T(8,128)(2,1)S(1)} %get-tuple-element.72), channel_id=1, source_target_pairs={{0,2},{1,3},{2,0},{3,1},{4,6},{5,7},{6,4},{7,5},{8,10},{9,11},{10,... | collective-permute-start | bytes 393224 | tf_op jit(solution)/shard_map/ppermute | solution.py:29
  105.1 1.8 %collective-permute-done.48.refs_2_ = bf16[128,512]{1,0:T(8,128)(2,1)S(1)} collective-permute-done((bf16[128,512]{1,0:T(8,128)(2,1)S(1)}, bf16[128,512]{1,0:T(8,128)(2,1)S(1)}, u32[]{:S(2)}, u32[]{:S(2)}) %collective-permute-start.48) | collective-permute-done | bytes 131104 | tf_op jit(solution)/shard_map/ppermute | solution.py:29
  (134 shorter events, 53.7 us)
Async XLA Ops:
  3.0 8.3 %collective-permute-start.2 = (bf16[128,512]{1,0:T(8,128)(2,1)S(1)}, bf16[128,512]{1,0:T(8,128)(2,1)S(1)}, u32[]{:S(2)}, u32[]{:S(2)}) collective-permute-start(bf16[128,512]{1,0:T(8,128)(2,1)S(1)} %shard_map.104.refs_0_.refs_3_), channel_id=1, source_target_pairs={{0,3},{1,2},{2,1},{3,0},{4,7},{5,6},{6,5},{7,4},{8,11},{9,10},{10,... | collective-permute-start | bytes 393224 | tf_op jit(solution)/shard_map/ppermute | solution.py:29
  7.0 6.6 %collective-permute-start.1 = (bf16[128,512]{1,0:T(8,128)(2,1)S(1)}, bf16[128,512]{1,0:T(8,128)(2,1)S(1)}, u32[]{:S(2)}, u32[]{:S(2)}) collective-permute-start(bf16[128,512]{1,0:T(8,128)(2,1)S(1)} %shard_map.104.refs_0_.refs_3_), channel_id=1, source_target_pairs={{0,1},{1,0},{2,3},{3,2},{4,5},{5,4},{6,7},{7,6},{8,9},{9,8},{10,11... | collective-permute-start | bytes 393224 | tf_op jit(solution)/shard_map/ppermute | solution.py:29
  7.5 6.0 %collective-permute-start = (bf16[128,512]{1,0:T(8,128)(2,1)S(1)}, bf16[128,512]{1,0:T(8,128)(2,1)S(1)}, u32[]{:S(2)}, u32[]{:S(2)}) collective-permute-start(bf16[128,512]{1,0:T(8,128)(2,1)S(1)} %shard_map.104.refs_0_.refs_3_), channel_id=1, source_target_pairs={{0,2},{1,3},{2,0},{3,1},{4,6},{5,7},{6,4},{7,5},{8,10},{9,11},{10,... | collective-permute-start | bytes 393224 | tf_op jit(solution)/shard_map/ppermute | solution.py:29
  14.4 5.6 %collective-permute-start.4 = (bf16[128,512]{1,0:T(8,128)(2,1)S(1)}, bf16[128,512]{1,0:T(8,128)(2,1)S(1)}, u32[]{:S(2)}, u32[]{:S(2)}) collective-permute-start(bf16[128,512]{1,0:T(8,128)(2,1)S(1)} %shard_map.111), channel_id=1, source_target_pairs={{0,1},{1,0},{2,3},{3,2},{4,5},{5,4},{6,7},{7,6},{8,9},{9,8},{10,11... | collective-permute-start | bytes 393224 | tf_op jit(solution)/shard_map/ppermute | solution.py:29
  16.3 6.1 %collective-permute-start.7 = (bf16[128,512]{1,0:T(8,128)(2,1)S(1)}, bf16[128,512]{1,0:T(8,128)(2,1)S(1)}, u32[]{:S(2)}, u32[]{:S(2)}) collective-permute-start(bf16[128,512]{1,0:T(8,128)(2,1)S(1)} %shard_map.112), channel_id=1, source_target_pairs={{0,2},{1,3},{2,0},{3,1},{4,6},{5,7},{6,4},{7,5},{8,10},{9,11},{10,... | collective-permute-start | bytes 393224 | tf_op jit(solution)/shard_map/ppermute | solution.py:29
  18.3 6.9 %collective-permute-start.6 = (bf16[128,512]{1,0:T(8,128)(2,1)S(1)}, bf16[128,512]{1,0:T(8,128)(2,1)S(1)}, u32[]{:S(2)}, u32[]{:S(2)}) collective-permute-start(bf16[128,512]{1,0:T(8,128)(2,1)S(1)} %get-tuple-element.46), channel_id=1, source_target_pairs={{0,2},{1,3},{2,0},{3,1},{4,6},{5,7},{6,4},{7,5},{8,10},{9,11},{10,... | collective-permute-start | bytes 393224 | tf_op jit(solution)/shard_map/ppermute | solution.py:29
  19.4 6.4 %collective-permute-start.3 = (bf16[128,512]{1,0:T(8,128)(2,1)S(1)}, bf16[128,512]{1,0:T(8,128)(2,1)S(1)}, u32[]{:S(2)}, u32[]{:S(2)}) collective-permute-start(bf16[128,512]{1,0:T(8,128)(2,1)S(1)} %get-tuple-element.44), channel_id=1, source_target_pairs={{0,1},{1,0},{2,3},{3,2},{4,5},{5,4},{6,7},{7,6},{8,9},{9,8},{10,11... | collective-permute-start | bytes 393224 | tf_op jit(solution)/shard_map/ppermute | solution.py:29
  20.0 6.9 %collective-permute-start.5 = (bf16[128,512]{1,0:T(8,128)(2,1)S(1)}, bf16[128,512]{1,0:T(8,128)(2,1)S(1)}, u32[]{:S(2)}, u32[]{:S(2)}) collective-permute-start(bf16[128,512]{1,0:T(8,128)(2,1)S(1)} %add_convert_fusion.7), channel_id=1, source_target_pairs={{0,2},{1,3},{2,0},{3,1},{4,6},{5,7},{6,4},{7,5},{8,10},{9,11},{10,... | collective-permute-start | bytes 393224 | tf_op jit(solution)/shard_map/ppermute | solution.py:29
  30.9 5.5 %collective-permute-start.10 = (bf16[128,256]{1,0:T(8,128)(2,1)S(1)}, bf16[128,256]{1,0:T(8,128)(2,1)S(1)}, u32[]{:S(2)}, u32[]{:S(2)}) collective-permute-start(bf16[128,256]{1,0:T(8,128)(2,1)S(1)} %add_convert_fusion.19), channel_id=1, source_target_pairs={{0,8},{4,12},{8,0},{12,4},{16,24},{20,28},{24,16},{28,20},{1,9},{5... | collective-permute-start | bytes 196616 | tf_op jit(solution)/shard_map/ppermute | solution.py:29
  33.7 5.6 %collective-permute-start.16 = (bf16[128,256]{1,0:T(8,128)(2,1)S(1)}, bf16[128,256]{1,0:T(8,128)(2,1)S(1)}, u32[]{:S(2)}, u32[]{:S(2)}) collective-permute-start(bf16[128,256]{1,0:T(8,128)(2,1)S(1)} %add_convert_fusion.15), channel_id=1, source_target_pairs={{0,16},{4,20},{8,24},{12,28},{16,0},{20,4},{24,8},{28,12},{1,17},{... | collective-permute-start | bytes 196616 | tf_op jit(solution)/shard_map/ppermute | solution.py:29
  36.4 5.6 %collective-permute-start.11 = (bf16[128,256]{1,0:T(8,128)(2,1)S(1)}, bf16[128,256]{1,0:T(8,128)(2,1)S(1)}, u32[]{:S(2)}, u32[]{:S(2)}) collective-permute-start(bf16[128,256]{1,0:T(8,128)(2,1)S(1)} %add_convert_fusion.18), channel_id=1, source_target_pairs={{0,16},{4,20},{8,24},{12,28},{16,0},{20,4},{24,8},{28,12},{1,17},{... | collective-permute-start | bytes 196616 | tf_op jit(solution)/shard_map/ppermute | solution.py:29
  48.4 6.0 %collective-permute-start.23 = (bf16[128,512]{1,0:T(8,128)(2,1)S(1)}, bf16[128,512]{1,0:T(8,128)(2,1)S(1)}, u32[]{:S(2)}, u32[]{:S(2)}) collective-permute-start(bf16[128,512]{1,0:T(8,128)(2,1)S(1)} %shard_map.118), channel_id=1, source_target_pairs={{0,1},{1,0},{2,3},{3,2},{4,5},{5,4},{6,7},{7,6},{8,9},{9,8},{10,11... | collective-permute-start | bytes 393224 | tf_op jit(solution)/shard_map/ppermute | solution.py:29
  49.3 6.9 %collective-permute-start.21 = (bf16[128,512]{1,0:T(8,128)(2,1)S(1)}, bf16[128,512]{1,0:T(8,128)(2,1)S(1)}, u32[]{:S(2)}, u32[]{:S(2)}) collective-permute-start(bf16[128,512]{1,0:T(8,128)(2,1)S(1)} %shard_map.117), channel_id=1, source_target_pairs={{0,2},{1,3},{2,0},{3,1},{4,6},{5,7},{6,4},{7,5},{8,10},{9,11},{10,... | collective-permute-start | bytes 393224 | tf_op jit(solution)/shard_map/ppermute | solution.py:29
  65.0 6.5 %collective-permute-start.26 = (bf16[128,256]{1,0:T(8,128)(2,1)S(1)}, bf16[128,256]{1,0:T(8,128)(2,1)S(1)}, u32[]{:S(2)}, u32[]{:S(2)}) collective-permute-start(bf16[128,256]{1,0:T(8,128)(2,1)S(1)} %add_convert_fusion.13), channel_id=1, source_target_pairs={{0,8},{4,12},{8,0},{12,4},{16,24},{20,28},{24,16},{28,20},{1,9},{5... | collective-permute-start | bytes 196616 | tf_op jit(solution)/shard_map/ppermute | solution.py:29
  67.5 8.3 %collective-permute-start.31 = (bf16[128,256]{1,0:T(8,128)(2,1)S(1)}, bf16[128,256]{1,0:T(8,128)(2,1)S(1)}, u32[]{:S(2)}, u32[]{:S(2)}) collective-permute-start(bf16[128,256]{1,0:T(8,128)(2,1)S(1)} %add_convert_fusion.9), channel_id=1, source_target_pairs={{0,16},{4,20},{8,24},{12,28},{16,0},{20,4},{24,8},{28,12},{1,17},{... | collective-permute-start | bytes 196616 | tf_op jit(solution)/shard_map/ppermute | solution.py:29
  71.5 5.7 %collective-permute-start.27 = (bf16[128,256]{1,0:T(8,128)(2,1)S(1)}, bf16[128,256]{1,0:T(8,128)(2,1)S(1)}, u32[]{:S(2)}, u32[]{:S(2)}) collective-permute-start(bf16[128,256]{1,0:T(8,128)(2,1)S(1)} %add_convert_fusion.12), channel_id=1, source_target_pairs={{0,16},{4,20},{8,24},{12,28},{16,0},{20,4},{24,8},{28,12},{1,17},{... | collective-permute-start | bytes 196616 | tf_op jit(solution)/shard_map/ppermute | solution.py:29
  83.1 6.4 %collective-permute-start.38 = (bf16[128,512]{1,0:T(8,128)(2,1)S(1)}, bf16[128,512]{1,0:T(8,128)(2,1)S(1)}, u32[]{:S(2)}, u32[]{:S(2)}) collective-permute-start(bf16[128,512]{1,0:T(8,128)(2,1)S(1)} %get-tuple-element.64.refs_0_), channel_id=1, source_target_pairs={{0,2},{1,3},{2,0},{3,1},{4,6},{5,7},{6,4},{7,5},{8,10},{9,11},{10,... | collective-permute-start | bytes 393224 | tf_op jit(solution)/shard_map/ppermute | solution.py:29
  83.9 6.4 %collective-permute-start.37 = (bf16[128,512]{1,0:T(8,128)(2,1)S(1)}, bf16[128,512]{1,0:T(8,128)(2,1)S(1)}, u32[]{:S(2)}, u32[]{:S(2)}) collective-permute-start(bf16[128,512]{1,0:T(8,128)(2,1)S(1)} %get-tuple-element.65.refs_1_), channel_id=1, source_target_pairs={{0,1},{1,0},{2,3},{3,2},{4,5},{5,4},{6,7},{7,6},{8,9},{9,8},{10,11... | collective-permute-start | bytes 393224 | tf_op jit(solution)/shard_map/ppermute | solution.py:29
  85.1 8.0 %collective-permute-start.39 = (bf16[128,512]{1,0:T(8,128)(2,1)S(1)}, bf16[128,512]{1,0:T(8,128)(2,1)S(1)}, u32[]{:S(2)}, u32[]{:S(2)}) collective-permute-start(bf16[128,512]{1,0:T(8,128)(2,1)S(1)} %get-tuple-element.64.refs_0_), channel_id=1, source_target_pairs={{0,1},{1,0},{2,3},{3,2},{4,5},{5,4},{6,7},{7,6},{8,9},{9,8},{10,11... | collective-permute-start | bytes 393224 | tf_op jit(solution)/shard_map/ppermute | solution.py:29
  86.0 7.2 %collective-permute-start.40 = (bf16[128,512]{1,0:T(8,128)(2,1)S(1)}, bf16[128,512]{1,0:T(8,128)(2,1)S(1)}, u32[]{:S(2)}, u32[]{:S(2)}) collective-permute-start(bf16[128,512]{1,0:T(8,128)(2,1)S(1)} %get-tuple-element.65.refs_1_), channel_id=1, source_target_pairs={{0,2},{1,3},{2,0},{3,1},{4,6},{5,7},{6,4},{7,5},{8,10},{9,11},{10,... | collective-permute-start | bytes 393224 | tf_op jit(solution)/shard_map/ppermute | solution.py:29
  96.0 5.5 %collective-permute-start.47 = (bf16[128,512]{1,0:T(8,128)(2,1)S(1)}, bf16[128,512]{1,0:T(8,128)(2,1)S(1)}, u32[]{:S(2)}, u32[]{:S(2)}) collective-permute-start(bf16[128,512]{1,0:T(8,128)(2,1)S(1)} %get-tuple-element.74), channel_id=1, source_target_pairs={{0,2},{1,3},{2,0},{3,1},{4,6},{5,7},{6,4},{7,5},{8,10},{9,11},{10,... | collective-permute-start | bytes 393224 | tf_op jit(solution)/shard_map/ppermute | solution.py:29
  97.4 6.4 %collective-permute-start.44 = (bf16[128,512]{1,0:T(8,128)(2,1)S(1)}, bf16[128,512]{1,0:T(8,128)(2,1)S(1)}, u32[]{:S(2)}, u32[]{:S(2)}) collective-permute-start(bf16[128,512]{1,0:T(8,128)(2,1)S(1)} %get-tuple-element.70), channel_id=1, source_target_pairs={{0,1},{1,0},{2,3},{3,2},{4,5},{5,4},{6,7},{7,6},{8,9},{9,8},{10,11... | collective-permute-start | bytes 393224 | tf_op jit(solution)/shard_map/ppermute | solution.py:29
  98.0 7.1 %collective-permute-start.46 = (bf16[128,512]{1,0:T(8,128)(2,1)S(1)}, bf16[128,512]{1,0:T(8,128)(2,1)S(1)}, u32[]{:S(2)}, u32[]{:S(2)}) collective-permute-start(bf16[128,512]{1,0:T(8,128)(2,1)S(1)} %get-tuple-element.72), channel_id=1, source_target_pairs={{0,2},{1,3},{2,0},{3,1},{4,6},{5,7},{6,4},{7,5},{8,10},{9,11},{10,... | collective-permute-start | bytes 393224 | tf_op jit(solution)/shard_map/ppermute | solution.py:29
  99.5 8.1 %collective-permute-start.43 = (bf16[128,512]{1,0:T(8,128)(2,1)S(1)}, bf16[128,512]{1,0:T(8,128)(2,1)S(1)}, u32[]{:S(2)}, u32[]{:S(2)}) collective-permute-start(bf16[128,512]{1,0:T(8,128)(2,1)S(1)} %get-tuple-element.68), channel_id=1, source_target_pairs={{0,1},{1,0},{2,3},{3,2},{4,5},{5,4},{6,7},{7,6},{8,9},{9,8},{10,11... | collective-permute-start | bytes 393224 | tf_op jit(solution)/shard_map/ppermute | solution.py:29
  (28 other events, 126.8 us)
